TPU v7x, 256 devices: a whole 4x4x8 slice. The times are simulated.
256 devices in a mesh: image: 16 (over z, core), dp: 16 (over y, x).
Axes of the slice: x: 4, y: 4, z: 8, core: 2. Of those that a mesh axis runs over, the one named last changes fastest.
Arguments:
- features: bfloat16 [16, 128, 128, 384], P('dp', 'image'), may hold values from -6 to 6
- conv_weight: bfloat16 [3, 3, 128, 128], replicated, may hold values from -0.1875 to 0.1875
- reduce_weight: bfloat16 [256, 128], replicated, may hold values from -0.375 to 0.375
- spectral_weight: bfloat16 [256, 256], replicated, may hold values from -0.375 to 0.375
- expand_weight: bfloat16 [128, 256], replicated, may hold values from -0.5 to 0.5
- upstream: bfloat16 [16, 128, 128, 384], P('dp', 'image'), may hold values from -6 to 6
Outputs:
- feature_grad: bfloat16 [16, 128, 128, 384], P('dp', 'image')
- conv_grad: float32 [3, 3, 128, 128], replicated
- reduce_grad: float32 [256, 128], replicated
- spectral_grad: float32 [256, 256], replicated
- expand_grad: float32 [128, 256], replicated
All inputs are finite; a program needn't handle non-finite values.
Results may differ from a plain program's by a relative error of at most 0.014.
Values may be sent and summed in bfloat16 or wider, within the bound.
No kernel may reach another device: no remote copies, remote signals or barrier semaphores. Data moves between devices by JAX's collectives and lax.ppermute only.
A program may use at most 64 MiB of HBM per device.

v0:
```python
import math

import jax
import jax.numpy as jnp
from jax import lax
from jax.sharding import Mesh
from jax.sharding import PartitionSpec as P

IMAGE = ("image_0", "image_1")
DP = ("dp_0", "dp_1")


def padded_2(block, sides, width):
    for axis, dim in sides:
        count = lax.axis_size(axis)
        forward = [(i, i + 1) for i in range(count - 1)]
        backward = [(target, source) for source, target in forward]
        low = lax.ppermute(
            lax.slice_in_dim(block, block.shape[dim] - width, None, axis=dim), axis, forward
        )
        high = lax.ppermute(lax.slice_in_dim(block, 0, width, axis=dim), axis, backward)
        block = jnp.concatenate([low, block, high], axis=dim)
    return block


def filled_up(lines, peers):
    spare = -len(lines) % peers
    return jnp.pad(lines, [(0, spare)] + [(0, 0)] * (lines.ndim - 1))


def copy_for_each(shard, axis):
    peers = lax.axis_size(axis)
    return lax.all_to_all(
        jnp.broadcast_to(shard[None], (peers, *shard.shape)), axis, 0, 0, tiled=True
    )


def joined_along(pieces, dim):
    dims = list(pieces.shape[1:])
    dims[dim] *= pieces.shape[0]
    return jnp.moveaxis(pieces, 0, dim).reshape(dims)


def gather_axes(shard, axes, dim):
    far, near = axes
    first = copy_for_each(shard, far)
    pieces = jnp.swapaxes(copy_for_each(first, near), 0, 1)
    return joined_along(pieces.reshape(-1, *shard.shape), dim)


def split_up(shard, dim, peers):
    dims = shard.shape
    pieces = shard.reshape(*dims[:dim], peers, dims[dim] // peers, *dims[dim + 1 :])
    return jnp.moveaxis(pieces, dim, 0)


def sum_at_owner(shard, axis, dim):
    pieces = split_up(shard, dim, lax.axis_size(axis))
    arrived = lax.all_to_all(pieces, axis, split_axis=0, concat_axis=0, tiled=True)
    return arrived.sum(axis=0)


def sum_by_axis(shard, axes, dim):
    far, near = axes
    own = sum_at_owner(split_up(shard, dim, lax.axis_size(far)), near, dim + 1)
    return jnp.sum(lax.all_to_all(own, far, 0, 0, tiled=True), axis=0)


def sum_by_parts(shard, axes):
    padded = filled_up(shard, lax.axis_size(axes[0]) * lax.axis_size(axes[1]))
    whole = gather_axes(sum_by_axis(padded, axes, 0), axes, 0)
    return lax.slice_in_dim(whole, 0, len(shard)).reshape(shard.shape)


def packed_total(arrays, axis):
    vector, at, outs = (jnp.concatenate([a.reshape(-1) for a in arrays]), 0, [])
    subtotal = sum_by_parts(vector, axis)
    for a in arrays:
        outs.append(subtotal[at : at + a.size].reshape(a.shape))
        at += a.size
    return tuple(outs)


def make_tables(length, number):
    lead = lax.broadcasted_iota(jnp.int32, (length, number), 0)
    trail = lax.broadcasted_iota(jnp.int32, (length, number), 1)
    angles = (lead * trail % length).astype(jnp.float32) * (2.0 * math.pi / length)
    factor = 1.0 / math.sqrt(length)
    return (
        (jnp.cos(angles) * factor).astype(jnp.bfloat16),
        (-jnp.sin(angles) * factor).astype(jnp.bfloat16),
    )


def inverse_tables(cosine, sine):
    number = cosine.shape[1]
    doubling = jnp.where(lax.broadcasted_iota(jnp.int32, (1, number), 1) == 0, 1.0, 2.0).astype(
        jnp.bfloat16
    )
    return ((cosine * doubling).T, (sine * doubling).T)


def product(form, left, right):
    return jnp.einsum(form, left, right, preferred_element_type=jnp.float32)


def halves(spectrum):
    half = spectrum.shape[-1] // 2
    return (spectrum[..., :half], spectrum[..., half:])


def height_forward(spectrum, cosine, sine):
    real_part, imag_part = halves(spectrum)
    out_real = product("hm,hkc->mkc", cosine, real_part) - product("hm,hkc->mkc", sine, imag_part)
    out_imag = product("hm,hkc->mkc", cosine, imag_part) + product("hm,hkc->mkc", sine, real_part)
    return jnp.concatenate([out_real, out_imag], axis=-1)


def height_inverse(spectrum, cosine, sine):
    real_part, imag_part = halves(spectrum)
    out_real = product("hm,mkc->hkc", cosine, real_part) + product("hm,mkc->hkc", sine, imag_part)
    out_imag = product("hm,mkc->hkc", cosine, imag_part) - product("hm,mkc->hkc", sine, real_part)
    return jnp.concatenate([out_real, out_imag], axis=-1)


def width_forward(hidden, cosine, sine):
    return jnp.concatenate(
        [product("hwc,wk->hkc", hidden, cosine), product("hwc,wk->hkc", hidden, sine)], axis=-1
    )


def width_forward_transpose(spectrum, cosine, sine):
    real_part, imag_part = halves(spectrum)
    return product("hkc,wk->hwc", real_part, cosine) + product("hkc,wk->hwc", imag_part, sine)


def width_inverse(spectrum, back_cos, back_sin):
    real_part, imag_part = halves(spectrum)
    return product("hkc,kw->hwc", real_part, back_cos) + product("hkc,kw->hwc", imag_part, back_sin)


def width_inverse_transpose(grad_map, back_cos, back_sin):
    return jnp.concatenate(
        [product("hwc,kw->hkc", grad_map, back_cos), product("hwc,kw->hkc", grad_map, back_sin)],
        axis=-1,
    )


def silu_slope(values):
    sigma = jax.nn.sigmoid(values)
    return sigma * (1.0 + values * (1.0 - sigma))


def conv_taps(padded, weights, row_count, col_count):
    summed = jnp.zeros((row_count * col_count, weights.shape[3]), jnp.float32)
    for tap_row in range(3):
        for tap_col in range(3):
            window = padded[tap_row : tap_row + row_count, tap_col : tap_col + col_count].reshape(
                row_count * col_count, -1
            )
            summed = summed + jnp.dot(
                window, weights[tap_row, tap_col], preferred_element_type=jnp.float32
            )
    return summed


def conv_back(padded, weights, row_count, col_count):
    summed = jnp.zeros((row_count * col_count, weights.shape[2]), jnp.float32)
    for tap_row in range(3):
        for tap_col in range(3):
            window = padded[
                2 - tap_row : 2 - tap_row + row_count, 2 - tap_col : 2 - tap_col + col_count
            ].reshape(row_count * col_count, -1)
            summed = summed + jnp.dot(
                window, weights[tap_row, tap_col].T, preferred_element_type=jnp.float32
            )
    return summed


def conv_grad_terms(padded, grad_flat, row_count, col_count):
    taps = []
    for tap_row in range(3):
        line = []
        for tap_col in range(3):
            window = padded[tap_row : tap_row + row_count, tap_col : tap_col + col_count].reshape(
                row_count * col_count, -1
            )
            line.append(product("pi,po->io", window, grad_flat))
        taps.append(jnp.stack(line))
    return jnp.stack(taps)


def shards(features, conv_weight, reduce_weight, spectral_weight, expand_weight, upstream):
    picture = features[0]
    incoming = upstream[0]
    row_count, breadth, channels = picture.shape
    local_count = conv_weight.shape[2]
    global_count, hidden_count = reduce_weight.shape
    groups = lax.axis_size(IMAGE)
    height = row_count * groups
    frequencies = breadth // 2
    cos_width, sin_width = make_tables(breadth, frequencies)
    cos_height, sin_height = make_tables(height, height)
    back_cos, back_sin = inverse_tables(cos_width, sin_width)
    x_local = picture[..., :local_count]
    x_global = picture[..., local_count:].reshape(-1, global_count)
    local_rows = padded_2(x_local, ((IMAGE, 0),), 1)
    local_pad = jnp.pad(local_rows, ((0, 0), (1, 1), (0, 0)))
    y_local = conv_taps(local_pad, conv_weight, row_count, breadth)
    pre_reduce = jnp.dot(x_global, reduce_weight, preferred_element_type=jnp.float32).reshape(
        row_count, breadth, hidden_count
    )
    hidden = jax.nn.silu(pre_reduce).astype(jnp.bfloat16)
    spectrum = width_forward(hidden, cos_width, sin_width).astype(jnp.bfloat16)
    columns = lax.all_to_all(spectrum, IMAGE, split_axis=1, concat_axis=0, tiled=True)
    column_spec = height_forward(columns, cos_height, sin_height).astype(jnp.bfloat16)
    flat_spec = column_spec.reshape(-1, 2 * hidden_count)
    pre_mix = jnp.dot(flat_spec, spectral_weight, preferred_element_type=jnp.float32)
    mixture = jax.nn.silu(pre_mix).astype(jnp.bfloat16).reshape(column_spec.shape)
    returned = height_inverse(mixture, cos_height, sin_height).astype(jnp.bfloat16)
    strip_spec = lax.all_to_all(returned, IMAGE, split_axis=0, concat_axis=1, tiled=True)
    spatial = width_inverse(strip_spec, back_cos, back_sin)
    combined = (hidden.astype(jnp.float32) + spatial).astype(jnp.bfloat16).reshape(-1, hidden_count)
    y_global = jnp.dot(combined, expand_weight, preferred_element_type=jnp.float32)
    y_all = jnp.concatenate([y_local, y_global], axis=-1)
    incoming_flat = incoming.reshape(-1, channels).astype(jnp.float32)
    d_pre = (incoming_flat * silu_slope(y_all)).astype(jnp.bfloat16)
    d_local = d_pre[:, :local_count]
    d_global = d_pre[:, local_count:]
    grad_local = conv_grad_terms(local_pad, d_local, row_count, breadth)
    d_rows = padded_2(d_local.reshape(row_count, breadth, local_count), ((IMAGE, 0),), 1)
    d_pad = jnp.pad(d_rows, ((0, 0), (1, 1), (0, 0)))
    dx_local = conv_back(d_pad, conv_weight, row_count, breadth)
    d_combined = jnp.dot(d_global, expand_weight.T, preferred_element_type=jnp.float32).astype(
        jnp.bfloat16
    )
    grad_expand = product("pi,po->io", combined, d_global)
    d_returned = width_inverse_transpose(
        d_combined.reshape(row_count, breadth, hidden_count), back_cos, back_sin
    ).astype(jnp.bfloat16)
    d_columns = lax.all_to_all(d_returned, IMAGE, split_axis=1, concat_axis=0, tiled=True)
    d_mixture = height_forward(d_columns, cos_height, sin_height)
    d_mix = (d_mixture.reshape(-1, 2 * hidden_count) * silu_slope(pre_mix)).astype(jnp.bfloat16)
    grad_spectral = product("pi,po->io", flat_spec, d_mix)
    d_column = (
        jnp.dot(d_mix, spectral_weight.T, preferred_element_type=jnp.float32)
        .astype(jnp.bfloat16)
        .reshape(column_spec.shape)
    )
    d_spectrum = height_inverse(d_column, cos_height, sin_height).astype(jnp.bfloat16)
    d_strip = lax.all_to_all(d_spectrum, IMAGE, split_axis=0, concat_axis=1, tiled=True)
    d_hidden = d_combined.reshape(row_count, breadth, hidden_count).astype(
        jnp.float32
    ) + width_forward_transpose(d_strip, cos_width, sin_width)
    d_reduce = (d_hidden * silu_slope(pre_reduce)).astype(jnp.bfloat16).reshape(-1, hidden_count)
    grad_reduce = product("pi,po->io", x_global, d_reduce)
    dx_global = jnp.dot(d_reduce, reduce_weight.T, preferred_element_type=jnp.float32)
    feature_grad = (incoming_flat + jnp.concatenate([dx_local, dx_global], axis=-1)).astype(
        jnp.bfloat16
    )
    grad_local, grad_reduce, grad_spectral, grad_expand = packed_total(
        (grad_local, grad_reduce, grad_spectral, grad_expand),
        (("image_0", "image_1", "dp_0"), "dp_1"),
    )
    factor = 1.0 / math.sqrt(lax.axis_size(DP) * height * breadth)
    return (
        feature_grad.reshape(1, row_count, breadth, channels),
        grad_local * factor,
        grad_reduce * factor,
        grad_spectral * factor,
        grad_expand * factor,
    )


def solution(mesh):
    split = Mesh(mesh.devices.reshape(8, 2, 4, 4), ("image_0", "image_1", "dp_0", "dp_1"))
    return jax.shard_map(
        shards,
        mesh=split,
        in_specs=(P(DP, IMAGE, None, None), P(), P(), P(), P(), P(DP, IMAGE, None, None)),
        out_specs=(P(DP, IMAGE, None, None), P(), P(), P(), P()),
        check_vma=False,
    )
```

profile of v0, /device:TPU:1, one launch (start us, length us, event | category | flops | bytes accessed | tf_op | source)
XLA Modules:
  0.0 205.1 jit_solution(10198412309161182714)
XLA Ops:
  0.6 0.8 fusion.282
  1.5 4.9 %collective-permute-start = (bf16[1,128,128]{2,1,0:T(8,128)(2,1)S(1)}, bf16[1,128,128]{2,1,0:T(8,128)(2,1)S(1)}, u32[]{:S(2)}, u32[]{:S(2)}) collective-permute-start(bf16[1,128,128]{2,1,0:T(8,128)(2,1)S(1)} %get-tuple-element.13), channel_id=1, source_target_pairs={{0,16},{16,32},{32,48},{48,64},{64,80},{80,96},{96,112},{112,128},... | collective-permute-start | bytes 98312 | tf_op jit(solution)/shard_map/ppermute | solution.py:18
  6.4 1.9 collective-permute-start.1
  8.3 2.1 %multiply_convert_fusion.3 = (bf16[8,128,128]{2,1,0:T(8,128)(2,1)S(1)}, f32[8,128,128]{2,1,0:T(8,128)}) fusion(bf16[256,128]{1,0:T(8,128)(2,1)} %param.8, bf16[8,128,384]{2,1,0:T(8,128)(2,1)} %bitcast.389), kind=kOutput, calls=%fused_computation.74 | convolution fusion | flops 67764224 | bytes 1376256 | tf_op jit(solution)/shard_map/dot_general | solution.py:210
  11.5 0.9 copy.89
  12.3 9.9 %all-to-all-start = ((bf16[8,64,256]{2,0,1:T(8,128)(2,1)}), bf16[8,64,256]{2,0,1:T(8,128)(2,1)}, u32[]{:S(2)}, u32[]{:S(2)}) async-start(bf16[8,64,256]{2,0,1:T(8,128)(2,1)} %copy.89), calls=%async_computation | async-start | bytes 524288 | tf_op jit(solution)/shard_map/all_to_all | solution.py:215
  22.2 1.0 slice.248
  27.6 1.1 convolution_add_fusion.11
  28.7 5.2 %all-to-all-done = bf16[8,64,256]{2,0,1:T(8,128)(2,1)} async-done(((bf16[8,64,256]{2,0,1:T(8,128)(2,1)}), bf16[8,64,256]{2,0,1:T(8,128)(2,1)}, u32[]{:S(2)}, u32[]{:S(2)}) %all-to-all-start) | async-done | bytes 262176 | tf_op jit(solution)/shard_map/all_to_all | solution.py:215
  33.9 1.0 copy.193
  37.0 1.0 multiply_convert_fusion.2
  40.3 0.9 copy.99
  41.2 3.4 %all-to-all-start.1 = ((bf16[128,4,256]{2,1,0:T(4,128)(2,1)}), bf16[128,4,256]{2,1,0:T(4,128)(2,1)S(1)}, u32[]{:S(2)}, u32[]{:S(2)}) async-start(bf16[128,4,256]{2,1,0:T(4,128)(2,1)} %copy.99), calls=%async_computation.1 | async-start | bytes 524288 | tf_op jit(solution)/shard_map/all_to_all | solution.py:221
  44.6 1.0 fusion.78
  45.7 2.1 %fusion.4 = f32[1024,128]{0,1:T(8,128)} fusion(f32[1024,128]{0,1:T(8,128)S(1)} %fusion.78, f32[1024,128]{0,1:T(8,128)} %convolution_add_fusion.11, bf16[1024,128]{1,0:T(8,128)(2,1)S(1)} %bitcast.325, bf16[3,3,128,128]{3,2,1,0:T(8,128)(2,1)} %param.7), kind=kOutput, calls=%fused_computation.27 | convolution fusion | flops 33816576 | bytes 1867776 | tf_op jit(solution)/shard_map/dot_general | solution.py:161
  47.8 8.0 %all-to-all-done.1 = bf16[128,4,256]{2,1,0:T(4,128)(2,1)S(1)} async-done(((bf16[128,4,256]{2,1,0:T(4,128)(2,1)}), bf16[128,4,256]{2,1,0:T(4,128)(2,1)S(1)}, u32[]{:S(2)}, u32[]{:S(2)}) %all-to-all-start.1) | async-done | bytes 262176 | tf_op jit(solution)/shard_map/all_to_all | solution.py:221
  56.0 0.8 all_to_all.75
  56.8 1.3 fusion.54
  58.1 1.3 fusion.12
  59.4 1.2 fusion.287
  61.3 0.9 convolution_bitcast_fusion.12
  62.1 0.9 convolution_bitcast_fusion.11
  63.0 0.9 convolution_bitcast_fusion.8
  66.7 1.9 collective-permute-start.2
  68.7 3.1 %collective-permute-start.3 = (bf16[1,128,128]{1,2,0:T(8,128)(2,1)}, bf16[1,128,128]{1,2,0:T(8,128)(2,1)}, u32[]{:S(2)}, u32[]{:S(2)}) collective-permute-start(bf16[1,128,128]{1,2,0:T(8,128)(2,1)} %get-tuple-element.12), channel_id=1, source_target_pairs={{16,0},{32,16},{48,32},{64,48},{80,64},{96,80},{112,96},{128,112},... | collective-permute-start | bytes 98312 | tf_op jit(solution)/shard_map/ppermute | solution.py:21
  71.8 0.9 copy.106
  72.7 4.9 %all-to-all-start.2 = ((bf16[8,64,256]{2,0,1:T(8,128)(2,1)}), bf16[8,64,256]{2,0,1:T(8,128)(2,1)S(1)}, u32[]{:S(2)}, u32[]{:S(2)}) async-start(bf16[8,64,256]{2,0,1:T(8,128)(2,1)} %copy.106), calls=%async_computation.2 | async-start | bytes 524288 | tf_op jit(solution)/shard_map/all_to_all | solution.py:241
  77.9 0.9 convolution_bitcast_fusion.9
  78.7 0.9 convolution_bitcast_fusion.7
  79.6 9.5 %all-to-all-done.2 = bf16[8,64,256]{2,0,1:T(8,128)(2,1)S(1)} async-done(((bf16[8,64,256]{2,0,1:T(8,128)(2,1)}), bf16[8,64,256]{2,0,1:T(8,128)(2,1)S(1)}, u32[]{:S(2)}, u32[]{:S(2)}) %all-to-all-start.2) | async-done | bytes 262176 | tf_op jit(solution)/shard_map/all_to_all | solution.py:241
  95.2 0.9 copy.113
  96.0 3.4 %all-to-all-start.3 = ((bf16[128,4,256]{2,1,0:T(4,128)(2,1)}), bf16[128,4,256]{2,1,0:T(4,128)(2,1)S(1)}, u32[]{:S(2)}, u32[]{:S(2)}) async-start(bf16[128,4,256]{2,1,0:T(4,128)(2,1)} %copy.113), calls=%async_computation.3 | async-start | bytes 524288 | tf_op jit(solution)/shard_map/all_to_all | solution.py:251
  99.6 1.2 convolution_bitcast_fusion.1
  100.9 9.7 %all-to-all-done.3 = bf16[128,4,256]{2,1,0:T(4,128)(2,1)S(1)} async-done(((bf16[128,4,256]{2,1,0:T(4,128)(2,1)}), bf16[128,4,256]{2,1,0:T(4,128)(2,1)S(1)}, u32[]{:S(2)}, u32[]{:S(2)}) %all-to-all-start.3) | async-done | bytes 262176 | tf_op jit(solution)/shard_map/all_to_all | solution.py:251
  111.3 1.6 fusion.11
  113.8 0.9 reshape_reshape.6
  114.7 1.1 copy.119
  115.8 4.0 %all-to-all-start.4 = ((f32[4,64,1088]{2,1,0:T(8,128)}), f32[4,64,1088]{2,1,0:T(8,128)S(1)}, u32[]{:S(2)}, u32[]{:S(2)}) async-start(f32[4,64,1088]{2,1,0:T(8,128)} %copy.119), calls=%async_computation.4 | async-start | bytes 2359296 | tf_op jit(solution)/shard_map/all_to_all | solution.py:59
  119.9 0.8 copy.102
  120.7 0.8 copy.103
  121.6 1.1 pad_maximum_fusion.4
  122.6 1.0 fusion.20
  123.6 1.5 fusion.281
  125.1 1.1 fusion.46
  126.2 10.0 %all-to-all-done.4 = f32[4,64,1088]{2,1,0:T(8,128)S(1)} async-done(((f32[4,64,1088]{2,1,0:T(8,128)}), f32[4,64,1088]{2,1,0:T(8,128)S(1)}, u32[]{:S(2)}, u32[]{:S(2)}) %all-to-all-start.4) | async-done | bytes 1114144 | tf_op jit(solution)/shard_map/all_to_all | solution.py:59
  136.3 0.9 all_to_all.85
  137.2 7.0 %all-to-all-start.5 = ((f32[64,1,1088]{2,1,0:T(1,128)}), f32[64,1,1088]{2,1,0:T(1,128)S(1)}, u32[]{:S(2)}, u32[]{:S(2)}) async-start(f32[64,1,1088]{2,1,0:T(1,128)} %all_to_all.85), calls=%async_computation.5 | async-start | bytes 589824 | tf_op jit(solution)/shard_map/all_to_all | solution.py:66
  144.2 1.2 convolution_add_fusion.8
  146.0 11.0 %all-to-all-done.5 = f32[64,1,1088]{2,1,0:T(1,128)S(1)} async-done(((f32[64,1,1088]{2,1,0:T(1,128)}), f32[64,1,1088]{2,1,0:T(1,128)S(1)}, u32[]{:S(2)}, u32[]{:S(2)}) %all-to-all-start.5) | async-done | bytes 278560 | tf_op jit(solution)/shard_map/all_to_all | solution.py:66
  157.3 0.9 broadcast_in_dim.24
  158.1 6.3 %all-to-all-start.6 = ((f32[64,1,1088]{2,1,0:T(1,128)}), f32[64,1,1088]{2,1,0:T(1,128)S(1)}, u32[]{:S(2)}, u32[]{:S(2)}) async-start(f32[64,1,1088]{2,1,0:T(1,128)} %broadcast_in_dim.24), calls=%async_computation.6 | async-start | bytes 589824 | tf_op jit(solution)/shard_map/all_to_all | solution.py:33
  165.2 12.2 %all-to-all-done.6 = f32[64,1,1088]{2,1,0:T(1,128)S(1)} async-done(((f32[64,1,1088]{2,1,0:T(1,128)}), f32[64,1,1088]{2,1,0:T(1,128)S(1)}, u32[]{:S(2)}, u32[]{:S(2)}) %all-to-all-start.6) | async-done | bytes 278560 | tf_op jit(solution)/shard_map/all_to_all | solution.py:33
  177.4 1.1 broadcast_in_dim.26
  178.5 3.5 %all-to-all-start.7 = ((f32[4,64,1088]{2,1,0:T(8,128)}), f32[4,64,1088]{2,1,0:T(8,128)S(1)}, u32[]{:S(2)}, u32[]{:S(2)}) async-start(f32[4,64,1088]{2,1,0:T(8,128)} %broadcast_in_dim.26), calls=%async_computation.7 | async-start | bytes 2359296 | tf_op jit(solution)/shard_map/all_to_all | solution.py:33
  182.4 1.3 convolution_add_fusion.1
  184.0 1.1 fusion.1
  185.1 11.6 %all-to-all-done.7 = f32[4,64,1088]{2,1,0:T(8,128)S(1)} async-done(((f32[4,64,1088]{2,1,0:T(8,128)}), f32[4,64,1088]{2,1,0:T(8,128)S(1)}, u32[]{:S(2)}, u32[]{:S(2)}) %all-to-all-start.7) | async-done | bytes 1114144 | tf_op jit(solution)/shard_map/all_to_all | solution.py:33
  196.7 0.8 copy.120
  197.4 0.9 slice.244
  199.0 0.7 slice_multiply_fusion.1
  199.7 2.0 slice.242
  201.7 1.0 reshape_reshape.7
  202.7 1.6 slice_multiply_fusion.3
  204.3 0.9 slice_multiply_fusion
  (181 shorter events, 23.7 us)
Async XLA Ops:
  0.6 36.4 %copy-start = (bf16[256,256]{1,0:T(8,128)(2,1)S(1)}, bf16[256,256]{1,0:T(8,128)(2,1)}, u32[]{:S(2)}) copy-start(bf16[256,256]{1,0:T(8,128)(2,1)} %param.9) | copy-start | bytes 393220
  1.5 22.0 %collective-permute-start = (bf16[1,128,128]{2,1,0:T(8,128)(2,1)S(1)}, bf16[1,128,128]{2,1,0:T(8,128)(2,1)S(1)}, u32[]{:S(2)}, u32[]{:S(2)}) collective-permute-start(bf16[1,128,128]{2,1,0:T(8,128)(2,1)S(1)} %get-tuple-element.13), channel_id=1, source_target_pairs={{0,16},{16,32},{32,48},{48,64},{64,80},{80,96},{96,112},{112,128},... | collective-permute-start | bytes 98312 | tf_op jit(solution)/shard_map/ppermute | solution.py:18
  6.4 17.1 %collective-permute-start.1 = (bf16[1,128,128]{2,1,0:T(8,128)(2,1)S(1)}, bf16[1,128,128]{2,1,0:T(8,128)(2,1)S(1)}, u32[]{:S(2)}, u32[]{:S(2)}) collective-permute-start(bf16[1,128,128]{2,1,0:T(8,128)(2,1)S(1)} %get-tuple-element.14), channel_id=1, source_target_pairs={{16,0},{32,16},{48,32},{64,48},{80,64},{96,80},{112,96},{128,112},... | collective-permute-start | bytes 98312 | tf_op jit(solution)/shard_map/ppermute | solution.py:21
  10.5 0.7 copy-start.11
  10.5 12.8 %copy-start.1 = (bf16[1,8,128,384]{3,2,1,0:T(8,128)(2,1)S(1)}, bf16[1,8,128,384]{3,2,1,0:T(8,128)(2,1)}, u32[]{:S(2)}) copy-start(bf16[1,8,128,384]{3,2,1,0:T(8,128)(2,1)} %param.11) | copy-start | bytes 2359300
  12.3 21.6 %all-to-all-start = ((bf16[8,64,256]{2,0,1:T(8,128)(2,1)}), bf16[8,64,256]{2,0,1:T(8,128)(2,1)}, u32[]{:S(2)}, u32[]{:S(2)}) async-start(bf16[8,64,256]{2,0,1:T(8,128)(2,1)} %copy.89), calls=%async_computation | async-start | bytes 524288 | tf_op jit(solution)/shard_map/all_to_all | solution.py:215
  23.5 0.6 copy-start.36
  24.1 0.6 copy-start.38
  24.9 1.0 copy-start.16
  24.9 1.2 copy-start.37
  24.9 1.2 copy-start.39
  25.2 1.5 copy-start.7
  25.2 1.5 copy-start.5
  25.2 2.1 %copy-start.3 = (bf16[8,128,128]{2,1,0:T(8,128)(2,1)}, bf16[8,128,128]{2,1,0:T(8,128)(2,1)S(1)}, u32[]{:S(2)}) copy-start(bf16[8,128,128]{2,1,0:T(8,128)(2,1)S(1)} %get-tuple-element.16) | copy-start | bytes 786436
  25.2 2.4 %copy-start.9 = (bf16[8,128,128]{2,1,0:T(8,128)(2,1)}, bf16[8,128,128]{2,1,0:T(8,128)(2,1)S(1)}, u32[]{:S(2)}) copy-start(bf16[8,128,128]{2,1,0:T(8,128)(2,1)S(1)} %get-tuple-element.15) | copy-start | bytes 786436
  26.2 0.9 copy-start.13
  36.4 1.6 copy-start.33
  37.0 1.1 copy-start.35
  41.2 14.6 %all-to-all-start.1 = ((bf16[128,4,256]{2,1,0:T(4,128)(2,1)}), bf16[128,4,256]{2,1,0:T(4,128)(2,1)S(1)}, u32[]{:S(2)}, u32[]{:S(2)}) async-start(bf16[128,4,256]{2,1,0:T(4,128)(2,1)} %copy.99), calls=%async_computation.1 | async-start | bytes 524288 | tf_op jit(solution)/shard_map/all_to_all | solution.py:221
  47.8 10.3 %copy-start.12 = (bf16[8,128,128]{2,1,0:T(8,128)(2,1)S(1)}, bf16[8,128,128]{2,1,0:T(8,128)(2,1)}, u32[]{:S(2)}) copy-start(bf16[8,128,128]{2,1,0:T(8,128)(2,1)} %copy-done.11) | copy-start | bytes 786436
  56.8 3.9 %copy-start.15 = (f32[1024,128]{0,1:T(8,128)S(1)}, f32[1024,128]{0,1:T(8,128)}, u32[]{:S(2)}) copy-start(f32[1024,128]{0,1:T(8,128)} %fusion.4) | copy-start | bytes 1572868
  60.6 1.5 copy-start.14
  61.2 2.7 %copy-start.10 = (bf16[8,128,128]{2,1,0:T(8,128)(2,1)S(1)}, bf16[8,128,128]{2,1,0:T(8,128)(2,1)}, u32[]{:S(2)}) copy-start(bf16[8,128,128]{2,1,0:T(8,128)(2,1)} %copy-done.9) | copy-start | bytes 786436
  63.0 2.7 %copy-start.32 = (bf16[128,256]{1,0:T(8,128)(2,1)S(1)}, bf16[128,256]{1,0:T(8,128)(2,1)}, u32[]{:S(2)}) copy-start(bf16[128,256]{1,0:T(8,128)(2,1)} %param.10) | copy-start | bytes 196612
  66.0 11.5 %copy-start.8 = (bf16[8,128,128]{2,1,0:T(8,128)(2,1)S(1)}, bf16[8,128,128]{2,1,0:T(8,128)(2,1)}, u32[]{:S(2)}) copy-start(bf16[8,128,128]{2,1,0:T(8,128)(2,1)} %copy-done.7) | copy-start | bytes 786436
  66.3 11.5 %copy-start.6 = (bf16[8,128,128]{2,1,0:T(8,128)(2,1)S(1)}, bf16[8,128,128]{2,1,0:T(8,128)(2,1)}, u32[]{:S(2)}) copy-start(bf16[8,128,128]{2,1,0:T(8,128)(2,1)} %copy-done.5) | copy-start | bytes 786436
  66.7 53.2 %collective-permute-start.2 = (bf16[1,128,128]{1,2,0:T(8,128)(2,1)}, bf16[1,128,128]{1,2,0:T(8,128)(2,1)}, u32[]{:S(2)}, u32[]{:S(2)}) collective-permute-start(bf16[1,128,128]{1,2,0:T(8,128)(2,1)} %get-tuple-element.11), channel_id=1, source_target_pairs={{0,16},{16,32},{32,48},{48,64},{64,80},{80,96},{96,112},{112,128},... | collective-permute-start | bytes 98312 | tf_op jit(solution)/shard_map/ppermute | solution.py:18
  68.7 10.1 %copy-start.4 = (bf16[8,128,128]{2,1,0:T(8,128)(2,1)S(1)}, bf16[8,128,128]{2,1,0:T(8,128)(2,1)}, u32[]{:S(2)}) copy-start(bf16[8,128,128]{2,1,0:T(8,128)(2,1)} %copy-done.3) | copy-start | bytes 786436
  68.7 52.1 %collective-permute-start.3 = (bf16[1,128,128]{1,2,0:T(8,128)(2,1)}, bf16[1,128,128]{1,2,0:T(8,128)(2,1)}, u32[]{:S(2)}, u32[]{:S(2)}) collective-permute-start(bf16[1,128,128]{1,2,0:T(8,128)(2,1)} %get-tuple-element.12), channel_id=1, source_target_pairs={{16,0},{32,16},{48,32},{64,48},{80,64},{96,80},{112,96},{128,112},... | collective-permute-start | bytes 98312 | tf_op jit(solution)/shard_map/ppermute | solution.py:21
  72.7 16.5 %all-to-all-start.2 = ((bf16[8,64,256]{2,0,1:T(8,128)(2,1)}), bf16[8,64,256]{2,0,1:T(8,128)(2,1)S(1)}, u32[]{:S(2)}, u32[]{:S(2)}) async-start(bf16[8,64,256]{2,0,1:T(8,128)(2,1)} %copy.106), calls=%async_computation.2 | async-start | bytes 524288 | tf_op jit(solution)/shard_map/all_to_all | solution.py:241
  91.3 1.0 copy-start.26
  94.6 4.9 %copy-start.29 = (f32[1,128,128]{2,1,0:T(8,128)S(1)}, f32[1,128,128]{2,1,0:T(8,128)}, u32[]{:S(2)}) copy-start(f32[1,128,128]{2,1,0:T(8,128)} %convolution_bitcast_fusion.8) | copy-start | bytes 196612
  94.6 4.9 %copy-start.30 = (f32[1,128,128]{2,1,0:T(8,128)S(1)}, f32[1,128,128]{2,1,0:T(8,128)}, u32[]{:S(2)}) copy-start(f32[1,128,128]{2,1,0:T(8,128)} %convolution_bitcast_fusion.9) | copy-start | bytes 196612
  94.6 4.9 %copy-start.31 = (f32[1,128,128]{2,1,0:T(8,128)S(1)}, f32[1,128,128]{2,1,0:T(8,128)}, u32[]{:S(2)}) copy-start(f32[1,128,128]{2,1,0:T(8,128)} %convolution_bitcast_fusion.7) | copy-start | bytes 196612
  95.0 4.5 %copy-start.27 = (f32[1,128,128]{2,1,0:T(8,128)S(1)}, f32[1,128,128]{2,1,0:T(8,128)}, u32[]{:S(2)}) copy-start(f32[1,128,128]{2,1,0:T(8,128)} %convolution_bitcast_fusion.12) | copy-start | bytes 196612
  95.0 4.5 %copy-start.28 = (f32[1,128,128]{2,1,0:T(8,128)S(1)}, f32[1,128,128]{2,1,0:T(8,128)}, u32[]{:S(2)}) copy-start(f32[1,128,128]{2,1,0:T(8,128)} %convolution_bitcast_fusion.11) | copy-start | bytes 196612
  95.1 4.5 %copy-start.34 = (bf16[128,4,128]{2,1,0:T(4,128)(2,1)S(1)}, bf16[128,4,128]{2,1,0:T(4,128)(2,1)}, u32[]{:S(2)}) copy-start(bf16[128,4,128]{2,1,0:T(4,128)(2,1)} %copy-done.33) | copy-start | bytes 393220
  96.0 14.6 %all-to-all-start.3 = ((bf16[128,4,256]{2,1,0:T(4,128)(2,1)}), bf16[128,4,256]{2,1,0:T(4,128)(2,1)S(1)}, u32[]{:S(2)}, u32[]{:S(2)}) async-start(bf16[128,4,256]{2,1,0:T(4,128)(2,1)} %copy.113), calls=%async_computation.3 | async-start | bytes 524288 | tf_op jit(solution)/shard_map/all_to_all | solution.py:251
  111.3 1.7 copy-start.25
  113.0 0.7 copy-start.18
  115.8 20.4 %all-to-all-start.4 = ((f32[4,64,1088]{2,1,0:T(8,128)}), f32[4,64,1088]{2,1,0:T(8,128)S(1)}, u32[]{:S(2)}, u32[]{:S(2)}) async-start(f32[4,64,1088]{2,1,0:T(8,128)} %copy.119), calls=%async_computation.4 | async-start | bytes 2359296 | tf_op jit(solution)/shard_map/all_to_all | solution.py:59
  125.1 19.1 %copy-start.17 = (bf16[3,3,128,128]{3,2,1,0:T(8,128)(2,1)S(1)}, bf16[3,3,128,128]{3,2,1,0:T(8,128)(2,1)}, u32[]{:S(2)}) copy-start(bf16[3,3,128,128]{3,2,1,0:T(8,128)(2,1)} %param.7) | copy-start | bytes 884740
  137.2 8.2 %copy-start.24 = (bf16[8,128,128]{1,0,2:T(8,128)(2,1)S(1)}, bf16[8,128,128]{1,0,2:T(8,128)(2,1)}, u32[]{:S(2)}) copy-start(bf16[8,128,128]{1,0,2:T(8,128)(2,1)} %get-tuple-element.9) | copy-start | bytes 786436
  137.2 8.5 %copy-start.23 = (bf16[8,128,128]{1,0,2:T(8,128)(2,1)S(1)}, bf16[8,128,128]{1,0,2:T(8,128)(2,1)}, u32[]{:S(2)}) copy-start(bf16[8,128,128]{1,0,2:T(8,128)(2,1)} %get-tuple-element.8) | copy-start | bytes 786436
  137.2 19.8 %all-to-all-start.5 = ((f32[64,1,1088]{2,1,0:T(1,128)}), f32[64,1,1088]{2,1,0:T(1,128)S(1)}, u32[]{:S(2)}, u32[]{:S(2)}) async-start(f32[64,1,1088]{2,1,0:T(1,128)} %all_to_all.85), calls=%async_computation.5 | async-start | bytes 589824 | tf_op jit(solution)/shard_map/all_to_all | solution.py:66
  146.0 18.7 %copy-start.22 = (bf16[8,128,128]{1,0,2:T(8,128)(2,1)S(1)}, bf16[8,128,128]{1,0,2:T(8,128)(2,1)}, u32[]{:S(2)}) copy-start(bf16[8,128,128]{1,0,2:T(8,128)(2,1)} %get-tuple-element.7) | copy-start | bytes 786436
  158.1 6.8 %copy-start.21 = (bf16[8,128,128]{1,0,2:T(8,128)(2,1)S(1)}, bf16[8,128,128]{1,0,2:T(8,128)(2,1)}, u32[]{:S(2)}) copy-start(bf16[8,128,128]{1,0,2:T(8,128)(2,1)} %get-tuple-element.6) | copy-start | bytes 786436
  158.1 19.2 %all-to-all-start.6 = ((f32[64,1,1088]{2,1,0:T(1,128)}), f32[64,1,1088]{2,1,0:T(1,128)S(1)}, u32[]{:S(2)}, u32[]{:S(2)}) async-start(f32[64,1,1088]{2,1,0:T(1,128)} %broadcast_in_dim.24), calls=%async_computation.6 | async-start | bytes 589824 | tf_op jit(solution)/shard_map/all_to_all | solution.py:33
  177.4 4.7 %copy-start.20 = (bf16[8,128,128]{1,0,2:T(8,128)(2,1)S(1)}, bf16[8,128,128]{1,0,2:T(8,128)(2,1)}, u32[]{:S(2)}) copy-start(bf16[8,128,128]{1,0,2:T(8,128)(2,1)} %get-tuple-element.21) | copy-start | bytes 786436
  178.5 18.1 %all-to-all-start.7 = ((f32[4,64,1088]{2,1,0:T(8,128)}), f32[4,64,1088]{2,1,0:T(8,128)S(1)}, u32[]{:S(2)}, u32[]{:S(2)}) async-start(f32[4,64,1088]{2,1,0:T(8,128)} %broadcast_in_dim.26), calls=%async_computation.7 | async-start | bytes 2359296 | tf_op jit(solution)/shard_map/all_to_all | solution.py:33
  182.1 1.6 copy-start.19
  182.1 1.6 copy-start.40
  182.4 1.6 copy-start.2
where the time goes:
time: 208 us; the launch traced here: 205 us
  waiting for transfers between devices  77.2 us (37%)
  starting transfers between devices  54.3 us (26%)
  matrix products  36 us (17%)
  local copies, waits for them, and re-layouts  27 us (13%)
  other arithmetic  8.65 us (4%)
    all_to_all x2, waiting for transfers between devices, copy_for_each(): lax.all_to_all(jnp.broadcast_to(shard[None], (peers, *shard.shape)), axis...  23.7 us
    dot_general x24, matrix products, product(): return jnp.einsum(form, left, right, preferred_element_type=jnp.float32)  14.8 us
    all_to_all x1, waiting for transfers between devices, sum_by_axis(): return jnp.sum(lax.all_to_all(own, far, 0, 0, tiled=True), axis=0)  11 us
    all_to_all x1, waiting for transfers between devices, sum_at_owner(): lax.all_to_all(pieces, axis, split_axis=0, concat_axis=0, tiled=True)  10 us
    all_to_all x1, starting transfers between devices, shards(): lax.all_to_all(spectrum, IMAGE, split_axis=1, concat_axis=0, tiled=True)  9.9 us
    all_to_all x2, starting transfers between devices, copy_for_each(): lax.all_to_all(jnp.broadcast_to(shard[None], (peers, *shard.shape)), axis...  9.8 us
    all_to_all x1, waiting for transfers between devices, shards(): lax.all_to_all(d_spectrum, IMAGE, split_axis=0, concat_axis=1, tiled=True)  9.66 us
    all_to_all x1, waiting for transfers between devices, shards(): lax.all_to_all(d_returned, IMAGE, split_axis=1, concat_axis=0, tiled=True)  9.52 us
  transfers between devices with their start and end apart: 12, of which 8 were waited for; matrix products, arithmetic and copies ran while one was open for 18% of the time, Pallas kernels for 0%

commit v1 on v0

v1 whole, which is shorter than its diff:
```python
import math

import jax
import jax.numpy as jnp
import numpy as np
from jax import lax
from jax.experimental import pallas as pl
from jax.experimental.pallas import tpu as pltpu
from jax.sharding import PartitionSpec as P

BF = jnp.bfloat16
F32 = jnp.float32
PEERS = 16
ROWS = 8
BREADTH = 128
CELLS = ROWS * BREADTH
LANES = 128
OWNED = 4
HALF = ROWS // 2


def width_table():
    w = np.arange(BREADTH)
    freq = np.arange(PEERS * OWNED).reshape(PEERS, OWNED)
    phase = (w[None, None, :] * freq[:, :, None] % BREADTH) * (2.0 * math.pi / BREADTH)
    factor = 1.0 / math.sqrt(BREADTH)
    base = np.stack([np.cos(phase) * factor, -np.sin(phase) * factor], axis=2)
    table = np.einsum("jkrw,hg->kjhrgw", base, np.eye(HALF))
    return table.reshape(OWNED * PEERS * HALF * 2, HALF * BREADTH).astype(BF)


def height_table():
    height = PEERS * ROWS
    h = np.arange(height)
    phase = (h[:, None] * h[None, :] % height) * (2.0 * math.pi / height)
    factor = 1.0 / math.sqrt(height)
    cosine, sine = np.cos(phase) * factor, -np.sin(phase) * factor
    table = np.zeros((2, height, height, 2))
    table[0, :, :, 0] = cosine.T
    table[0, :, :, 1] = -sine.T
    table[1, :, :, 1] = cosine.T
    table[1, :, :, 0] = sine.T
    return table.reshape(2 * height, 2 * height).astype(BF)


def dot(left, right):
    return jnp.dot(left, right, preferred_element_type=F32)


def dot_t(left, right):
    return lax.dot_general(left, right, (((1,), (1,)), ((), ())), preferred_element_type=F32)


def slope_of(values, sigma):
    return sigma * (1.0 + values * (1.0 - sigma))


def to_owners(cells, table):
    side = jnp.concatenate([cells[: CELLS // 2], cells[CELLS // 2 :]], axis=1)
    found = dot(table, side)
    parts = [
        found[:, q * LANES : (q + 1) * LANES].reshape(OWNED, PEERS, ROWS, LANES) for q in range(2)
    ]
    joined = jnp.concatenate(parts, axis=2).astype(BF)
    return [joined[k] for k in range(OWNED)]


def from_owners(strip, table_t):
    wide = strip.astype(F32)
    halves = []
    for q in range(2):
        piece = wide[:, q * ROWS : (q + 1) * ROWS, :]
        rows = [
            piece[:, :, k * LANES : (k + 1) * LANES].reshape(PEERS * ROWS, LANES)
            for k in range(OWNED)
        ]
        halves.append(jnp.concatenate(rows, axis=0).astype(BF))
    found = dot(table_t, jnp.concatenate(halves, axis=1))
    return jnp.concatenate([found[:, :LANES], found[:, LANES:]], axis=0)


def by_frequency(columns):
    height = columns.shape[0] // 2
    return jnp.concatenate(
        [
            jnp.concatenate(
                [
                    columns[:height, k * LANES : (k + 1) * LANES],
                    columns[height:, k * LANES : (k + 1) * LANES],
                ],
                axis=1,
            )
            for k in range(OWNED)
        ],
        axis=0,
    )


def by_part(mixed):
    height = mixed.shape[0] // OWNED
    return jnp.concatenate(
        [
            jnp.concatenate(
                [
                    mixed[k * height : (k + 1) * height, r * LANES : (r + 1) * LANES]
                    for k in range(OWNED)
                ],
                axis=1,
            )
            for r in range(2)
        ],
        axis=0,
    )


def doubling():
    lane = lax.broadcasted_iota(jnp.int32, (1, OWNED * LANES), 1)
    return jnp.where((lane < LANES) & (lax.axis_index("image") == 0), 1.0, 2.0)


def forward_rows(x, u, weight, table, spec, hidden, slope, first, last):
    pre = dot(x[:, LANES:], weight[...])
    sigma = jax.nn.sigmoid(pre)
    low = (pre * sigma).astype(BF)
    hidden[...] = low
    for k, block in enumerate(to_owners(low, table[...])):
        spec[:, :, k * LANES : (k + 1) * LANES] = block
    slope[...] = slope_of(pre, sigma)
    first[: 2 * BREADTH] = x[: 2 * BREADTH, :LANES]
    first[2 * BREADTH :] = u[:BREADTH, :LANES]
    last[: 2 * BREADTH] = x[CELLS - 2 * BREADTH :, :LANES]
    last[2 * BREADTH :] = u[CELLS - BREADTH :, :LANES]


def local_part(x, u, above, below, weight, grad, terms):
    rows = jnp.concatenate([above[: 2 * BREADTH], x[:, :LANES], below[: 2 * BREADTH]], axis=0)

    def beside(cells):
        wide = cells.astype(F32)
        count = wide.shape[0]
        column = lax.broadcasted_iota(jnp.int32, wide.shape, 0) % BREADTH
        before = jnp.where(column == 0, 0.0, pltpu.roll(wide, 1, 0)).astype(BF)
        after = jnp.where(column == BREADTH - 1, 0.0, pltpu.roll(wide, count - 1, 0)).astype(BF)
        return before, after

    before, after = beside(rows)
    x3 = jnp.concatenate([before, rows, after], axis=1)
    y = jnp.zeros((CELLS + 2 * BREADTH, LANES), F32)
    for a in range(3):
        y = y + dot(
            x3[a * BREADTH : a * BREADTH + CELLS + 2 * BREADTH],
            weight[a * 3 * LANES : (a + 1) * 3 * LANES],
        )
    incoming = jnp.concatenate([above[2 * BREADTH :], u[:, :LANES], below[2 * BREADTH :]], axis=0)
    d = (incoming.astype(F32) * slope_of(y, jax.nn.sigmoid(y))).astype(BF)
    before, after = beside(d)
    d3 = jnp.concatenate([after, d, before], axis=1)
    dx = u[:, :LANES].astype(F32)
    for a in range(3):
        taps = [weight[(3 * a + b) * LANES : (3 * a + b + 1) * LANES] for b in range(3)]
        dx = dx + dot_t(
            d3[(2 - a) * BREADTH : (2 - a) * BREADTH + CELLS], jnp.concatenate(taps, axis=1)
        )
    grad[...] = dx.astype(BF)
    d_t = d[BREADTH : BREADTH + CELLS].T
    for a in range(3):
        found = dot(d_t, x3[(a + 1) * BREADTH : (a + 1) * BREADTH + CELLS])
        terms[a * 3 * LANES : (a + 1) * 3 * LANES] = found.T.astype(BF)


def columns_forward(arrived, table, table_t, weight, sent, flat, slope):
    columns = arrived[...].reshape(PEERS * ROWS * 2, OWNED * LANES)
    spec = by_frequency(dot(table[...], columns).astype(BF))
    flat[...] = spec
    pre = dot(spec, weight[...])
    sigma = jax.nn.sigmoid(pre)
    back = dot(table_t[...], by_part((pre * sigma).astype(BF)))
    sent[...] = (back * doubling()).astype(BF).reshape(sent.shape)
    slope[...] = slope_of(pre, sigma)


def middle_rows(arrived, hidden, u, weight, table, table_t, *outs):
    sent, d_combined, combined, d_global = outs
    spatial = from_owners(arrived[...], table_t[...])
    mix = (hidden[...].astype(F32) + spatial).astype(BF)
    combined[...] = mix
    y = dot(mix, weight[...])
    incoming = u[:, LANES:].astype(F32)
    d = (incoming * slope_of(y, jax.nn.sigmoid(y))).astype(BF)
    d_global[...] = d
    back = dot_t(d, weight[...]).astype(BF)
    d_combined[...] = back
    for k, block in enumerate(to_owners(back, table[...])):
        sent[:, :, k * LANES : (k + 1) * LANES] = block


def columns_backward(arrived, table, table_t, weight, slope, sent, d_mix):
    columns = arrived[...].reshape(PEERS * ROWS * 2, OWNED * LANES)
    found = by_frequency(dot(table[...], columns) * doubling())
    d = (found * slope[...]).astype(BF)
    d_mix[...] = d
    back = dot(table_t[...], by_part(dot_t(d, weight[...]).astype(BF)))
    sent[...] = back.astype(BF).reshape(sent.shape)


def last_rows(arrived, d_combined, slope, x_t, table_t, other, d_reduce, terms):
    d_hidden = d_combined[...].astype(F32) + from_owners(arrived[...], table_t[...])
    d = (d_hidden * slope[...]).astype(BF)
    d_reduce[...] = d
    terms[:, :16] = dot(x_t[...], d).astype(BF).reshape(PEERS, 16, LANES)
    terms[:, 16:] = other[...]


def transposed(x, x_t):
    x_t[...] = x[:, LANES:].T


def expand_terms(combined, d_global, terms):
    found = dot(combined[...].T, d_global[...])
    terms[...] = jnp.concatenate([found[:, :LANES], found[:, LANES:]], axis=0).astype(BF)


def spectral_terms(flat, d_mix, expand, conv, terms):
    found = dot(flat[...].T, d_mix[...])
    both = jnp.concatenate([found[:, :LANES], found[:, LANES:]], axis=0).astype(BF)
    terms[:, :32] = both.reshape(PEERS, 32, LANES)
    terms[:, 32:48] = expand[...].reshape(PEERS, 16, LANES)
    terms[:, 48:] = conv[...].reshape(PEERS, 72, LANES)


def global_grad(d_reduce, weight, u, local, out):
    out[:, :LANES] = local[...]
    out[:, LANES:] = (u[:, LANES:].astype(F32) + dot_t(d_reduce[...], weight[...])).astype(BF)


def summed(arrived, sent):
    total = jnp.sum(arrived[...].astype(F32), axis=0).astype(BF)
    sent[...] = jnp.broadcast_to(total[None], sent.shape)


def unpacked(factor, arrived, conv, reduce, spectral, expand):
    found = arrived[...].astype(F32) * factor
    reduce[...] = found[:, :16].reshape(256, LANES)
    both = found[:, 16:48].reshape(512, LANES)
    spectral[:, :LANES] = both[:256]
    spectral[:, LANES:] = both[256:]
    both = found[:, 48:64].reshape(256, LANES)
    expand[:, :LANES] = both[:128]
    expand[:, LANES:] = both[128:]
    conv[...] = found[:, 64:].reshape(9 * LANES, LANES)


WHOLE = pl.BlockSpec(memory_space=pltpu.VMEM)


def run(body, outs, *args, name=None, cost=4):
    many = isinstance(outs[0][0], tuple)
    return pl.pallas_call(
        body,
        out_shape=tuple(jax.ShapeDtypeStruct(*o) for o in outs)
        if many
        else jax.ShapeDtypeStruct(*outs),
        in_specs=[WHOLE] * len(args),
        out_specs=(WHOLE,) * len(outs) if many else WHOLE,
        name=name,
        cost_estimate=pl.CostEstimate(
            flops=int(cost * 1e8), bytes_accessed=1 << 20, transcendentals=0
        ),
        compiler_params=pltpu.CompilerParams(vmem_limit_bytes=24 << 20),
    )(*args)


def exchange(array, axis):
    return lax.all_to_all(array, axis, 0, 0, tiled=True)


def shards(features, conv_weight, reduce_weight, spectral_weight, expand_weight, upstream):
    x = features.reshape(CELLS, 3 * LANES)
    u = upstream.reshape(CELLS, 3 * LANES)
    conv = conv_weight.reshape(9 * LANES, LANES)
    width = width_table()
    height = height_table()
    wide, wide_t = jnp.asarray(width), jnp.asarray(np.ascontiguousarray(width.T))
    tall, tall_t = jnp.asarray(height), jnp.asarray(np.ascontiguousarray(height.T))
    message = ((PEERS, 2 * ROWS, OWNED * LANES), BF)
    cells = ((CELLS, LANES), BF)
    edge = ((3 * BREADTH, LANES), BF)

    spec, hidden, slope, first, last = run(
        forward_rows,
        (message, cells, ((CELLS, LANES), F32), edge, edge),
        *(x, u, reduce_weight, wide),
        name="forward_rows",
    )
    arrived = exchange(spec, "image")
    forward = [(i, i + 1) for i in range(PEERS - 1)]
    backward = [(b, a) for a, b in forward]
    above = lax.ppermute(last, "image", forward)
    below = lax.ppermute(first, "image", backward)
    local, conv_terms = run(
        local_part,
        (cells, ((9 * LANES, LANES), BF)),
        *(x, u, above, below, conv),
        name="local_part",
        cost=30,
    )
    sent, flat, mix_slope = run(
        columns_forward,
        (message, ((512, 256), BF), ((512, 256), F32)),
        *(arrived, tall, tall_t, spectral_weight),
        name="columns_forward",
    )
    arrived = exchange(sent, "image")
    x_t = run(
        transposed,
        ((256, CELLS), BF),
        x,
        name="transposed",
        cost=10,
    )
    sent, d_combined, combined, d_global = run(
        middle_rows,
        (message, cells, cells, ((CELLS, 256), BF)),
        *(arrived, hidden, u, expand_weight, wide, wide_t),
        name="middle_rows",
    )
    arrived = exchange(sent, "image")
    expand = run(expand_terms, ((256, LANES), BF), combined, d_global, name="expand_terms", cost=10)
    sent, d_mix = run(
        columns_backward,
        (message, ((512, 256), BF)),
        *(arrived, tall, tall_t, spectral_weight, mix_slope),
        name="columns_backward",
    )
    arrived = exchange(sent, "image")
    other = run(
        spectral_terms,
        ((PEERS, 120, LANES), BF),
        *(flat, d_mix, expand, conv_terms),
        name="spectral_terms",
        cost=10,
    )
    packed = ((PEERS, 136, LANES), BF)
    d_reduce, terms = run(
        last_rows,
        (cells, packed),
        *(arrived, d_combined, slope, x_t, wide_t, other),
        name="last_rows",
    )
    arrived = exchange(terms, "dp")
    grad = run(
        global_grad,
        ((CELLS, 3 * LANES), BF),
        *(d_reduce, reduce_weight, u, local),
        name="global_grad",
        cost=10,
    )
    arrived = exchange(run(summed, packed, arrived, name="sum_images"), "image")
    arrived = exchange(run(summed, packed, arrived, name="sum_strips"), "dp")
    factor = 1.0 / math.sqrt(PEERS * PEERS * ROWS * BREADTH)
    conv_sum, reduce_sum, spectral_sum, expand_sum = run(
        lambda *refs: unpacked(factor, *refs),
        (
            ((9 * LANES, LANES), F32),
            ((256, LANES), F32),
            ((256, 256), F32),
            ((128, 256), F32),
        ),
        arrived,
        name="unpacked",
    )
    return (
        grad.reshape(1, ROWS, BREADTH, 3 * LANES),
        conv_sum.reshape(3, 3, LANES, LANES),
        reduce_sum,
        spectral_sum,
        expand_sum,
    )


def solution(mesh):
    return jax.shard_map(
        shards,
        mesh=mesh,
        in_specs=(P("dp", "image", None, None), P(), P(), P(), P(), P("dp", "image", None, None)),
        out_specs=(P("dp", "image", None, None), P(), P(), P(), P()),
        check_vma=False,
    )
```

time: 208 us -> 140 us (0.67)
  blocking collectives: 0 us -> 76.3 us
  waiting for transfers between devices: 77.2 us -> 22.4 us
  starting transfers between devices: 54.3 us -> 15.6 us
  matrix products: 36 us -> 0 us
  local copies, waits for them, and re-layouts: 27 us -> 10.4 us
  Pallas kernels: 0 us -> 13.1 us
  other arithmetic: 8.65 us -> 0 us
    all_to_all x0 -> x4, blocking collectives: none -> 76.3 us  [exchange(): return lax.all_to_all(array, axis, 0, 0, tiled=True)]
    all_to_all x8 -> x3, waiting for transfers between devices: 77.2 us -> 22.4 us  [exchange(): return lax.all_to_all(array, axis, 0, 0, tiled=True)]
    all_to_all x8 -> x3, starting transfers between devices: 42.4 us -> 10.6 us  [exchange(): return lax.all_to_all(array, axis, 0, 0, tiled=True)]
    dot_general x48 -> x0, matrix products: 31 us -> none  [the longest x24 14.8 us: product(): return jnp.einsum(form, left, right, preferred_element_type=jnp.float32)]
    pallas_call x0 -> x13, Pallas kernels: none -> 13.1 us  [run(): pl.pallas_call(body, out_shape=tuple((jax.ShapeDtypeStruct(*o) for o in o...]
    slice x10 -> x0, local copies, waits for them, and re-layouts: 7.37 us -> none  [the longest x2 2.9 us: packed_total(): outs.append(subtotal[at:at + a.size].reshape(a.shape))]
    ppermute x4 -> x2, starting transfers between devices: 11.9 us -> 5 us  [the longest x1 3.07 us: shards(): above = lax.ppermute(last, 'image', forward)]
    unnamed x93 -> x60, local copies, waits for them, and re-layouts: 4.42 us -> 10.4 us
  transfers between devices with their start and end apart: 12 -> 5, of which waited for: 8 -> 3; matrix products, arithmetic and copies ran while one was open for 18% -> 0% of each run, Pallas kernels for 0% -> 5%
where the time goes in v1:
time: 140 us; the launch traced here: 139 us
  blocking collectives  76.3 us (54%)
  waiting for transfers between devices  22.4 us (16%)
  starting transfers between devices  15.6 us (11%)
  Pallas kernels  13.1 us (9%)
  local copies, waits for them, and re-layouts  10.4 us (7%)
    all_to_all x4, blocking collectives, exchange(): return lax.all_to_all(array, axis, 0, 0, tiled=True)  76.3 us
    all_to_all x3, waiting for transfers between devices, exchange(): return lax.all_to_all(array, axis, 0, 0, tiled=True)  22.4 us
    pallas_call x13, Pallas kernels, run(): pl.pallas_call(body, out_shape=tuple((jax.ShapeDtypeStruct(*o) for o in o...  13.1 us
    all_to_all x3, starting transfers between devices, exchange(): return lax.all_to_all(array, axis, 0, 0, tiled=True)  10.6 us
    unnamed x60, local copies, waits for them, and re-layouts  10.4 us
    ppermute x1, starting transfers between devices, shards(): above = lax.ppermute(last, 'image', forward)  3.07 us
  transfers between devices with their start and end apart: 5, of which 3 were waited for; matrix products, arithmetic and copies ran while one was open for 0% of the time, Pallas kernels for 5%

profile of v1, /device:TPU:1, one launch (start us, length us, event | category | flops | bytes accessed | tf_op | source)
XLA Modules:
  0.0 138.7 jit_solution(14696582030523809548)
XLA Ops:
  0.6 0.0 copy-start
  0.6 1.1 copy-done
  1.8 1.0 copy-done.3
  2.8 1.1 copy-done.5
  3.9 0.8 copy-done.10
  4.8 1.3 forward_rows.1
  6.1 21.5 %all_to_all.35.arrived = bf16[16,16,512]{2,1,0:T(8,128)(2,1)S(1)} all-to-all(bf16[16,16,512]{2,1,0:T(8,128)(2,1)S(1)} %get-tuple-element.27), channel_id=1, replica_groups=mesh['image'=16,'dp'=16] {'image'}, dimensions={0} | all-to-all | bytes 524288 | tf_op jit(solution)/shard_map/all_to_all | solution.py:274
  27.6 0.0 copy-done.19
  27.6 0.0 copy-done.20
  27.6 0.0 copy-done.21
  27.6 0.0 copy-start.1
  27.6 0.0 copy-start.4
  27.6 0.0 copy-start.9
  27.6 0.7 columns_forward.1
  28.3 0.0 copy-start.22
  28.3 0.8 copy-done.22
  29.1 14.5 %all_to_all.36.arrived = bf16[16,16,512]{2,1,0:T(8,128)(2,1)S(1)} all-to-all(bf16[16,16,512]{2,1,0:T(8,128)(2,1)S(1)} %get-tuple-element.28), channel_id=1, replica_groups=mesh['image'=16,'dp'=16] {'image'}, dimensions={0} | all-to-all | bytes 524288 | tf_op jit(solution)/shard_map/all_to_all | solution.py:274
  43.6 0.0 copy-done.26
  43.6 0.0 copy-done.1
  43.6 0.0 copy-done.4
  43.6 0.0 copy-done.9
  43.6 0.0 copy-done.2
  43.6 2.0 %middle_rows.1 = (bf16[16,16,512]{2,1,0:T(8,128)(2,1)}, bf16[1024,128]{1,0:T(8,128)(2,1)S(1)}, bf16[1024,128]{1,0:T(8,128)(2,1)S(1)}, bf16[1024,256]{1,0:T(8,128)(2,1)S(1)}) custom-call(bf16[16,16,512]{2,1,0:T(8,128)(2,1)S(1)} %all_to_all.36.arrived, bf16[1024,128]{1,0:T(8,128)(2,1)S(1)} %get-tuple-element.29.hidden, bf16[1024,384]{1,0:T(8,128)(2,1)S(1)} %bitcast.6, ...), custom_call_target="tpu_custom_call" | custom-call | flops 400000000 | bytes 1048576 | tf_op jit(solution)/shard_map/middle_rows/pallas_call | solution.py:258
  45.6 0.7 copy-done.7
  46.3 0.7 copy-done.15
  47.0 3.4 %all-to-all-start.2 = ((bf16[16,16,512]{2,1,0:T(8,128)(2,1)}), bf16[16,16,512]{2,1,0:T(8,128)(2,1)S(1)}, u32[]{:S(2)}, u32[]{:S(2)}) async-start(bf16[16,16,512]{2,1,0:T(8,128)(2,1)} %get-tuple-element.30), calls=%async_computation.2 | async-start | bytes 524288 | tf_op jit(solution)/shard_map/all_to_all | solution.py:274
  50.5 3.1 %collective-permute-start = (bf16[384,128]{1,0:T(8,128)(2,1)}, bf16[384,128]{1,0:T(8,128)(2,1)}, u32[]{:S(2)}, u32[]{:S(2)}) collective-permute-start(bf16[384,128]{1,0:T(8,128)(2,1)} %get-tuple-element.39), channel_id=1, source_target_pairs={{0,16},{16,32},{32,48},{48,64},{64,80},{80,96},{96,112},{112,128},... | collective-permute-start | bytes 294920 | tf_op jit(solution)/shard_map/ppermute | solution.py:298
  53.6 1.9 %collective-permute-start.1 = (bf16[384,128]{1,0:T(8,128)(2,1)S(1)}, bf16[384,128]{1,0:T(8,128)(2,1)}, u32[]{:S(2)}, u32[]{:S(2)}) collective-permute-start(bf16[384,128]{1,0:T(8,128)(2,1)S(1)} %get-tuple-element.40), channel_id=1, source_target_pairs={{16,0},{32,16},{48,32},{64,48},{80,64},{96,80},{112,96},{128,112},... | collective-permute-start | bytes 294920 | tf_op jit(solution)/shard_map/ppermute | solution.py:299
  55.5 6.2 %all-to-all-done.2.arrived = bf16[16,16,512]{2,1,0:T(8,128)(2,1)S(1)} async-done(((bf16[16,16,512]{2,1,0:T(8,128)(2,1)}), bf16[16,16,512]{2,1,0:T(8,128)(2,1)S(1)}, u32[]{:S(2)}, u32[]{:S(2)}) %all-to-all-start.2) | async-done | bytes 262176 | tf_op jit(solution)/shard_map/all_to_all | solution.py:274
  61.7 0.0 copy-done.12
  61.7 1.0 copy-done.23
  62.8 1.4 columns_backward.1
  64.1 0.7 copy-done.24
  64.8 3.4 %all-to-all-start.3 = ((bf16[16,16,512]{2,1,0:T(8,128)(2,1)}), bf16[16,16,512]{2,1,0:T(8,128)(2,1)S(1)}, u32[]{:S(2)}, u32[]{:S(2)}) async-start(bf16[16,16,512]{2,1,0:T(8,128)(2,1)} %get-tuple-element.32), calls=%async_computation.3 | async-start | bytes 524288 | tf_op jit(solution)/shard_map/all_to_all | solution.py:274
  68.3 0.0 copy-done.6
  68.3 0.0 copy-start.14
  68.3 0.2 transposed.1.x_t
  68.5 0.0 collective-permute-done.above
  68.5 0.0 collective-permute-done.1.below
  68.5 0.7 copy-done.14
  69.2 3.1 %local_part.1 = (bf16[1024,128]{1,0:T(8,128)(2,1)S(1)}, bf16[1152,128]{1,0:T(8,128)(2,1)S(1)}) custom-call(bf16[1024,384]{1,0:T(8,128)(2,1)S(1)} %bitcast.11, bf16[1024,384]{1,0:T(8,128)(2,1)S(1)} %bitcast.7, bf16[384,128]{1,0:T(8,128)(2,1)} %collective-permute-done.above, bf16[384,128]{1,0:T(8,128)(2,1)} %collective-permute-done.1.below, ...), custom_call_target="tpu_custom_call" | custom-call | flops 3000000000 | bytes 1048576 | tf_op jit(solution)/shard_map/local_part/pallas_call | solution.py:258
  72.3 0.0 copy-start.28
  72.4 0.0 copy-done.13
  72.4 0.0 copy-done.16
  72.4 0.0 copy-start.25
  72.4 0.0 copy-start.27
  72.4 0.3 expand_terms.1.expand
  72.7 0.4 copy-done.28
  73.1 0.4 copy-done.25
  73.4 0.1 copy-done.27
  73.5 0.3 spectral_terms.1.other
  73.8 6.1 %all-to-all-done.3.arrived = bf16[16,16,512]{2,1,0:T(8,128)(2,1)S(1)} async-done(((bf16[16,16,512]{2,1,0:T(8,128)(2,1)}), bf16[16,16,512]{2,1,0:T(8,128)(2,1)S(1)}, u32[]{:S(2)}, u32[]{:S(2)}) %all-to-all-start.3) | async-done | bytes 262176 | tf_op jit(solution)/shard_map/all_to_all | solution.py:274
  79.9 0.0 copy-done.8
  79.9 0.7 last_rows.1
  80.6 0.0 copy-start.17
  80.6 0.7 copy-done.17
  81.3 18.7 %all_to_all.37.arrived = bf16[16,136,128]{2,1,0:T(8,128)(2,1)S(1)} all-to-all(bf16[16,136,128]{2,1,0:T(8,128)(2,1)S(1)} %get-tuple-element.44), channel_id=1, replica_groups=mesh['image'=16,'dp'=16] {'dp'}, dimensions={0} | all-to-all | bytes 1114112 | tf_op jit(solution)/shard_map/all_to_all | solution.py:274
  100.0 0.1 sum_images.1
  100.1 21.7 %all_to_all.38.arrived = bf16[16,136,128]{2,1,0:T(8,128)(2,1)S(1)} all-to-all(bf16[16,136,128]{2,1,0:T(8,128)(2,1)S(1)} %sum_images.1), channel_id=1, replica_groups=mesh['image'=16,'dp'=16] {'image'}, dimensions={0} | all-to-all | bytes 1114112 | tf_op jit(solution)/shard_map/all_to_all | solution.py:274
  121.8 0.9 sum_strips.1
  122.7 3.7 %all-to-all-start.6 = ((bf16[16,136,128]{2,1,0:T(8,128)(2,1)}), bf16[16,136,128]{2,1,0:T(8,128)(2,1)S(1)}, u32[]{:S(2)}, u32[]{:S(2)}) async-start(bf16[16,136,128]{2,1,0:T(8,128)(2,1)} %sum_strips.1), calls=%async_computation.6 | async-start | bytes 1114112 | tf_op jit(solution)/shard_map/all_to_all | solution.py:274
  126.4 1.2 global_grad.1
  127.6 10.0 %all-to-all-done.6.refs_0_ = bf16[16,136,128]{2,1,0:T(8,128)(2,1)S(1)} async-done(((bf16[16,136,128]{2,1,0:T(8,128)(2,1)}), bf16[16,136,128]{2,1,0:T(8,128)(2,1)S(1)}, u32[]{:S(2)}, u32[]{:S(2)}) %all-to-all-start.6) | async-done | bytes 557088 | tf_op jit(solution)/shard_map/all_to_all | solution.py:274
  137.7 1.0 unpacked.1
  (23 shorter events, 0.0 us)
Async XLA Ops:
  0.6 1.1 copy-start
  1.8 1.0 copy-start.3
  2.8 1.1 copy-start.5
  3.9 0.8 copy-start.10
  6.1 21.5 %copy-start.19 = (bf16[256,256]{1,0:T(8,128)(2,1)S(1)}, bf16[256,256]{1,0:T(8,128)(2,1)}, u32[]{:S(2)}) copy-start(bf16[256,256]{1,0:T(8,128)(2,1)} %weight.8) | copy-start | bytes 393220
  6.1 21.5 %copy-start.20 = (bf16[256,256]{1,0:T(8,128)(2,1)S(1)}, bf16[256,256]{1,0:T(8,128)(2,1)}, u32[]{:S(2)}) copy-start(bf16[256,256]{1,0:T(8,128)(2,1)} %constant.10.clone.table) | copy-start | bytes 393220
  6.1 21.5 %copy-start.21 = (bf16[256,256]{1,0:T(8,128)(2,1)S(1)}, bf16[256,256]{1,0:T(8,128)(2,1)}, u32[]{:S(2)}) copy-start(bf16[256,256]{1,0:T(8,128)(2,1)} %constant.11.clone.table_t) | copy-start | bytes 393220
  27.6 16.0 %copy-start.1 = (bf16[1,8,128,384]{3,2,1,0:T(8,128)(2,1)S(1)}, bf16[1,8,128,384]{3,2,1,0:T(8,128)(2,1)}, u32[]{:S(2)}) copy-start(bf16[1,8,128,384]{3,2,1,0:T(8,128)(2,1)} %param.15) | copy-start | bytes 2359300
  27.6 16.0 %copy-start.4 = (bf16[512,512]{1,0:T(8,128)(2,1)S(1)}, bf16[512,512]{1,0:T(8,128)(2,1)}, u32[]{:S(2)}) copy-start(bf16[512,512]{1,0:T(8,128)(2,1)} %constant.8.clone.table) | copy-start | bytes 1572868
  27.6 16.0 %copy-start.9 = (bf16[128,256]{1,0:T(8,128)(2,1)S(1)}, bf16[128,256]{1,0:T(8,128)(2,1)}, u32[]{:S(2)}) copy-start(bf16[128,256]{1,0:T(8,128)(2,1)} %weight.7) | copy-start | bytes 196612
  28.3 0.8 copy-start.22
  29.1 14.5 %copy-start.26 = (bf16[512,256]{1,0:T(8,128)(2,1)}, bf16[512,256]{1,0:T(8,128)(2,1)S(1)}, u32[]{:S(2)}) copy-start(bf16[512,256]{1,0:T(8,128)(2,1)S(1)} %get-tuple-element.35.flat) | copy-start | bytes 786436
  29.1 14.5 %copy-start.2 = (bf16[512,512]{1,0:T(8,128)(2,1)S(1)}, bf16[512,512]{1,0:T(8,128)(2,1)}, u32[]{:S(2)}) copy-start(bf16[512,512]{1,0:T(8,128)(2,1)} %constant.9.clone.table_t) | copy-start | bytes 1572868
  45.6 0.7 copy-start.7
  46.3 0.7 copy-start.15
  47.0 14.7 %copy-start.12 = (bf16[1024,256]{1,0:T(8,128)(2,1)}, bf16[1024,256]{1,0:T(8,128)(2,1)S(1)}, u32[]{:S(2)}) copy-start(bf16[1024,256]{1,0:T(8,128)(2,1)S(1)} %get-tuple-element.38.d_global) | copy-start | bytes 1572868
  47.0 14.7 %all-to-all-start.2 = ((bf16[16,16,512]{2,1,0:T(8,128)(2,1)}), bf16[16,16,512]{2,1,0:T(8,128)(2,1)S(1)}, u32[]{:S(2)}, u32[]{:S(2)}) async-start(bf16[16,16,512]{2,1,0:T(8,128)(2,1)} %get-tuple-element.30), calls=%async_computation.2 | async-start | bytes 524288 | tf_op jit(solution)/shard_map/all_to_all | solution.py:274
  50.5 18.0 %collective-permute-start = (bf16[384,128]{1,0:T(8,128)(2,1)}, bf16[384,128]{1,0:T(8,128)(2,1)}, u32[]{:S(2)}, u32[]{:S(2)}) collective-permute-start(bf16[384,128]{1,0:T(8,128)(2,1)} %get-tuple-element.39), channel_id=1, source_target_pairs={{0,16},{16,32},{32,48},{48,64},{64,80},{80,96},{96,112},{112,128},... | collective-permute-start | bytes 294920 | tf_op jit(solution)/shard_map/ppermute | solution.py:298
  53.6 14.9 %collective-permute-start.1 = (bf16[384,128]{1,0:T(8,128)(2,1)S(1)}, bf16[384,128]{1,0:T(8,128)(2,1)}, u32[]{:S(2)}, u32[]{:S(2)}) collective-permute-start(bf16[384,128]{1,0:T(8,128)(2,1)S(1)} %get-tuple-element.40), channel_id=1, source_target_pairs={{16,0},{32,16},{48,32},{64,48},{80,64},{96,80},{112,96},{128,112},... | collective-permute-start | bytes 294920 | tf_op jit(solution)/shard_map/ppermute | solution.py:299
  61.7 1.0 copy-start.23
  62.8 5.5 %copy-start.6 = (bf16[1,8,128,384]{3,2,1,0:T(8,128)(2,1)S(1)}, bf16[1,8,128,384]{3,2,1,0:T(8,128)(2,1)}, u32[]{:S(2)}) copy-start(bf16[1,8,128,384]{3,2,1,0:T(8,128)(2,1)} %param.10) | copy-start | bytes 2359300
  64.1 0.7 copy-start.24
  64.8 15.1 %all-to-all-start.3 = ((bf16[16,16,512]{2,1,0:T(8,128)(2,1)}), bf16[16,16,512]{2,1,0:T(8,128)(2,1)S(1)}, u32[]{:S(2)}, u32[]{:S(2)}) async-start(bf16[16,16,512]{2,1,0:T(8,128)(2,1)} %get-tuple-element.32), calls=%async_computation.3 | async-start | bytes 524288 | tf_op jit(solution)/shard_map/all_to_all | solution.py:274
  68.3 1.0 copy-start.14
  69.2 3.1 %copy-start.13 = (bf16[1024,256]{1,0:T(8,128)(2,1)S(1)}, bf16[1024,256]{1,0:T(8,128)(2,1)}, u32[]{:S(2)}) copy-start(bf16[1024,256]{1,0:T(8,128)(2,1)} %copy-done.12) | copy-start | bytes 1572868
  69.2 3.1 %copy-start.16 = (bf16[1024,128]{1,0:T(8,128)(2,1)S(1)}, bf16[1024,128]{1,0:T(8,128)(2,1)}, u32[]{:S(2)}) copy-start(bf16[1024,128]{1,0:T(8,128)(2,1)} %copy-done.15) | copy-start | bytes 786436
  72.3 0.7 copy-start.28
  72.4 1.0 copy-start.25
  72.4 1.1 copy-start.27
  73.5 6.4 %copy-start.8 = (bf16[1024,128]{1,0:T(8,128)(2,1)S(1)}, bf16[1024,128]{1,0:T(8,128)(2,1)}, u32[]{:S(2)}) copy-start(bf16[1024,128]{1,0:T(8,128)(2,1)} %copy-done.7) | copy-start | bytes 786436
  80.6 0.7 copy-start.17
  122.7 3.7 %copy-start.11 = (bf16[256,128]{1,0:T(8,128)(2,1)S(1)}, bf16[256,128]{1,0:T(8,128)(2,1)}, u32[]{:S(2)}) copy-start(bf16[256,128]{1,0:T(8,128)(2,1)} %weight.9) | copy-start | bytes 196612
  122.7 3.7 %copy-start.18 = (bf16[1024,128]{1,0:T(8,128)(2,1)S(1)}, bf16[1024,128]{1,0:T(8,128)(2,1)}, u32[]{:S(2)}) copy-start(bf16[1024,128]{1,0:T(8,128)(2,1)} %copy-done.17) | copy-start | bytes 786436
  122.7 3.7 %copy-start.29 = (bf16[1024,128]{1,0:T(8,128)(2,1)S(1)}, bf16[1024,128]{1,0:T(8,128)(2,1)}, u32[]{:S(2)}) copy-start(bf16[1024,128]{1,0:T(8,128)(2,1)} %copy-done.28) | copy-start | bytes 786436
  122.7 15.0 %all-to-all-start.6 = ((bf16[16,136,128]{2,1,0:T(8,128)(2,1)}), bf16[16,136,128]{2,1,0:T(8,128)(2,1)S(1)}, u32[]{:S(2)}, u32[]{:S(2)}) async-start(bf16[16,136,128]{2,1,0:T(8,128)(2,1)} %sum_strips.1), calls=%async_computation.6 | async-start | bytes 1114112 | tf_op jit(solution)/shard_map/all_to_all | solution.py:274

commit v2 on v1

v2 whole, which is shorter than its diff:
```python
import math

import jax
import jax.numpy as jnp
import numpy as np
from jax import lax
from jax.experimental import pallas as pl
from jax.experimental.pallas import tpu as pltpu
from jax.sharding import Mesh
from jax.sharding import PartitionSpec as P

BF = jnp.bfloat16
F32 = jnp.float32
PEERS = 16
ROWS = 8
BREADTH = 128
CELLS = ROWS * BREADTH
LANES = 128
OWNED = 4
HALF = ROWS // 2
SIDE = 4
LEVELS = 8
IMAGE = ("z", "core")
DP = ("y", "x")
CONV = 40
TERMS = 16 + 8 + CONV + 8


def width_table():
    w = np.arange(BREADTH)
    freq = np.arange(PEERS * OWNED).reshape(PEERS, OWNED)
    phase = (w[None, None, :] * freq[:, :, None] % BREADTH) * (2.0 * math.pi / BREADTH)
    factor = 1.0 / math.sqrt(BREADTH)
    base = np.stack([np.cos(phase) * factor, -np.sin(phase) * factor], axis=2)
    table = np.einsum("jkrw,hg->kjhrgw", base, np.eye(HALF))
    return table.reshape(OWNED * PEERS * HALF * 2, HALF * BREADTH).astype(BF)


def narrow_table():
    table = width_table().reshape(OWNED, PEERS, HALF, 2, HALF, BREADTH)
    return np.einsum("kjhrhw->kjhrw", table).reshape(-1, BREADTH)


def height_table():
    height = PEERS * ROWS
    h = np.arange(height)
    phase = (h[:, None] * h[None, :] % height) * (2.0 * math.pi / height)
    factor = 1.0 / math.sqrt(height)
    cosine, sine = np.cos(phase) * factor, -np.sin(phase) * factor
    table = np.zeros((2, height, height, 2))
    table[0, :, :, 0] = cosine.T
    table[0, :, :, 1] = -sine.T
    table[1, :, :, 1] = cosine.T
    table[1, :, :, 0] = sine.T
    return table.reshape(2 * height, 2 * height).astype(BF)


def dot(left, right):
    return jnp.dot(left, right, preferred_element_type=F32)


def dot_t(left, right):
    return lax.dot_general(left, right, (((1,), (1,)), ((), ())), preferred_element_type=F32)


def slope_of(values, sigma):
    return sigma * (1.0 + values * (1.0 - sigma))


def to_owners(cells, table):
    side = jnp.concatenate([cells[: CELLS // 2], cells[CELLS // 2 :]], axis=1)
    found = dot(table, side)
    parts = [
        found[:, q * LANES : (q + 1) * LANES].reshape(OWNED, PEERS, ROWS, LANES) for q in range(2)
    ]
    joined = jnp.concatenate(parts, axis=2).astype(BF)
    return [joined[k] for k in range(OWNED)]


def from_owners(strip, table_t):
    wide = strip.astype(F32)
    halves = []
    for q in range(2):
        rows = [
            wide[:, (2 * k + q) * ROWS : (2 * k + q + 1) * ROWS].reshape(PEERS * ROWS, LANES)
            for k in range(OWNED)
        ]
        halves.append(jnp.concatenate(rows, axis=0).astype(BF))
    found = dot(table_t, jnp.concatenate(halves, axis=1))
    return jnp.concatenate([found[:, :LANES], found[:, LANES:]], axis=0)


def store_message(sent, blocks):
    for k, block in enumerate(blocks):
        sent[:, 2 * k * ROWS : 2 * (k + 1) * ROWS] = block


def columns_of(arrived):
    return jnp.concatenate(
        [
            arrived[:, 2 * k * ROWS : 2 * (k + 1) * ROWS].reshape(PEERS * ROWS * 2, LANES)
            for k in range(OWNED)
        ],
        axis=1,
    )


def blocks_of(columns):
    return [
        columns[:, k * LANES : (k + 1) * LANES].reshape(PEERS, 2 * ROWS, LANES)
        for k in range(OWNED)
    ]


def by_frequency(columns):
    height = columns.shape[0] // 2
    return jnp.concatenate(
        [
            jnp.concatenate(
                [
                    columns[:height, k * LANES : (k + 1) * LANES],
                    columns[height:, k * LANES : (k + 1) * LANES],
                ],
                axis=1,
            )
            for k in range(OWNED)
        ],
        axis=0,
    )


def by_part(mixed):
    height = mixed.shape[0] // OWNED
    return jnp.concatenate(
        [
            jnp.concatenate(
                [
                    mixed[k * height : (k + 1) * height, r * LANES : (r + 1) * LANES]
                    for k in range(OWNED)
                ],
                axis=1,
            )
            for r in range(2)
        ],
        axis=0,
    )


def doubling():
    lane = lax.broadcasted_iota(jnp.int32, (1, OWNED * LANES), 1)
    first = lax.axis_index(IMAGE) == 0
    return jnp.where((lane < LANES) & first, 1.0, 2.0)


def started(copies, sems):
    made = [pltpu.make_async_copy(a, b, sems.at[i]) for i, (a, b) in enumerate(copies)]
    for copy in made:
        copy.start()
    return made


def forward_rows(x, u, weight, narrow, spec, hidden, slope, first, last, *scratch):
    held, near_weight, base, sems = scratch
    edge, local = 2 * BREADTH, pl.ds(0, LANES)
    copies = started(
        [
            (narrow, base),
            (weight, near_weight),
            (x.at[:, pl.ds(LANES, 2 * LANES)], held),
            (x.at[pl.ds(0, edge), local], first.at[pl.ds(0, edge)]),
            (x.at[pl.ds(CELLS - edge, edge), local], last.at[pl.ds(0, edge)]),
            (u.at[pl.ds(0, BREADTH), local], first.at[pl.ds(edge, BREADTH)]),
            (u.at[pl.ds(CELLS - BREADTH, BREADTH), local], last.at[pl.ds(edge, BREADTH)]),
        ],
        sems,
    )
    copies[0].wait()
    row = lax.broadcasted_iota(jnp.int32, (PEERS * OWNED * ROWS, BREADTH), 0) // 2 % HALF
    table = jnp.concatenate(
        [base[...] * (row == g).astype(F32).astype(BF) for g in range(HALF)], axis=1
    )
    copies[1].wait()
    copies[2].wait()
    pre = dot(held[...], near_weight[...])
    sigma = jax.nn.sigmoid(pre)
    low = (pre * sigma).astype(BF)
    hidden[...] = low
    store_message(spec, to_owners(low, table))
    slope[...] = slope_of(pre, sigma)
    for copy in copies[3:]:
        copy.wait()


def local_part(far_x, far_u, above, below, far_weight, grad, terms, x, u, weight, sems):
    local = (slice(None), pl.ds(0, LANES))
    copies = started([(far_x.at[local], x), (far_u.at[local], u), (far_weight, weight)], sems)
    for copy in copies:
        copy.wait()
    rows = jnp.concatenate([above[: 2 * BREADTH], x[...], below[: 2 * BREADTH]], axis=0)

    def beside(cells):
        wide = cells.astype(F32)
        count = wide.shape[0]
        column = lax.broadcasted_iota(jnp.int32, wide.shape, 0) % BREADTH
        before = jnp.where(column == 0, 0.0, pltpu.roll(wide, 1, 0)).astype(BF)
        after = jnp.where(column == BREADTH - 1, 0.0, pltpu.roll(wide, count - 1, 0)).astype(BF)
        return before, after

    before, after = beside(rows)
    x3 = jnp.concatenate([before, rows, after], axis=1)
    y = jnp.zeros((CELLS + 2 * BREADTH, LANES), F32)
    for a in range(3):
        y = y + dot(
            x3[a * BREADTH : a * BREADTH + CELLS + 2 * BREADTH],
            weight[a * 3 * LANES : (a + 1) * 3 * LANES],
        )
    incoming = jnp.concatenate([above[2 * BREADTH :], u[...], below[2 * BREADTH :]], axis=0)
    d = (incoming.astype(F32) * slope_of(y, jax.nn.sigmoid(y))).astype(BF)
    before, after = beside(d)
    d3 = jnp.concatenate([after, d, before], axis=1)
    dx = u[...].astype(F32)
    for a in range(3):
        taps = [weight[(3 * a + b) * LANES : (3 * a + b + 1) * LANES] for b in range(3)]
        dx = dx + dot_t(
            d3[(2 - a) * BREADTH : (2 - a) * BREADTH + CELLS], jnp.concatenate(taps, axis=1)
        )
    grad[...] = dx.astype(BF)
    d_t = d[BREADTH : BREADTH + CELLS].T
    for a in range(3):
        found = dot(d_t, x3[(a + 1) * BREADTH : (a + 1) * BREADTH + CELLS])
        terms[a * 3 * LANES : (a + 1) * 3 * LANES] = found.T.astype(BF)
    terms[9 * LANES :] = jnp.zeros((2 * PEERS * CONV - 9 * LANES, LANES), BF)


def columns_forward(arrived, table, table_t, weight, sent, flat, slope):
    spec = by_frequency(dot(table[...], columns_of(arrived)).astype(BF))
    flat[...] = spec
    pre = dot(spec, weight[...])
    sigma = jax.nn.sigmoid(pre)
    back = dot(table_t[...], by_part((pre * sigma).astype(BF)))
    store_message(sent, blocks_of((back * doubling()).astype(BF)))
    slope[...] = slope_of(pre, sigma)


def middle_rows(arrived, hidden, u, weight, table, table_t, sent, d_combined, expand):
    spatial = from_owners(arrived[...], table_t[...])
    mix = (hidden[...].astype(F32) + spatial).astype(BF)
    y = dot(mix, weight[...])
    incoming = u[:, LANES:].astype(F32)
    d = (incoming * slope_of(y, jax.nn.sigmoid(y))).astype(BF)
    back = dot_t(d, weight[...]).astype(BF)
    d_combined[...] = back
    store_message(sent, to_owners(back, table[...]))
    found = dot(mix.T, d)
    expand[...] = jnp.concatenate([found[:, :LANES], found[:, LANES:]], axis=0).astype(BF)


def columns_backward(arrived, table, table_t, weight, slope, flat, expand, conv, sent, terms):
    found = by_frequency(dot(table[...], columns_of(arrived)) * doubling())
    d = (found * slope[...]).astype(BF)
    back = dot(table_t[...], by_part(dot_t(d, weight[...]).astype(BF)))
    store_message(sent, blocks_of(back.astype(BF)))
    spectral = dot(flat[...].T, d)
    for c in range(2):
        part = spectral[:, c * LANES : (c + 1) * LANES].reshape(PEERS, 16, LANES)
        terms[c, :, :16] = part.astype(BF)
        part = expand[c * LANES : (c + 1) * LANES].astype(F32).reshape(PEERS, 8, LANES)
        terms[c, :, 16:24] = part.astype(BF)
        part = conv[c * PEERS * CONV : (c + 1) * PEERS * CONV].astype(F32)
        terms[c, :, 24:] = part.reshape(PEERS, CONV, LANES).astype(BF)


def last_rows(arrived, d_combined, slope, x, table_t, other, d_reduce, kept, sent, terms):
    d_hidden = d_combined[...].astype(F32) + from_owners(arrived[...], table_t[...])
    d = (d_hidden * slope[...]).astype(BF)
    d_reduce[...] = d
    found = dot(d.T, x[:, LANES:]).T
    terms[...] = found.reshape(2, PEERS, 8, LANES).astype(BF)
    me = lax.axis_index("core")
    for target, core in ((kept, me), (sent, 1 - me)):
        target[:, : TERMS - 8] = other[core]
        target[:, TERMS - 8 :] = terms[core]


def added(kept, other, out):
    out[...] = (kept[...].astype(F32) + other[...].astype(F32)).astype(BF)


def global_grad(d_reduce, weight, u, local, out):
    out[:, :LANES] = local[...]
    out[:, LANES:] = (u[:, LANES:].astype(F32) + dot_t(d_reduce[...], weight[...])).astype(BF)


def summed(arrived, sent):
    total = jnp.sum(arrived[...].astype(F32), axis=0).astype(BF)
    sent[...] = jnp.broadcast_to(total[None], sent.shape)


def unpacked(factor, mine, other, conv, reduce, spectral, expand, held):
    me = lax.axis_index("core")
    held[me] = mine[...]
    held[1 - me] = other[...]
    for c in range(2):
        found = held[c].astype(F32) * factor
        spectral[:, c * LANES : (c + 1) * LANES] = found[:, :16].reshape(256, LANES)
        expand[:, c * LANES : (c + 1) * LANES] = found[:, 16:24].reshape(LANES, LANES)
        begin = c * PEERS * CONV
        count = min(PEERS * CONV, 9 * LANES - begin)
        part = found[:, 24 : 24 + CONV].reshape(PEERS * CONV, LANES)
        conv[begin : begin + count] = part[:count]
        reduce[c * LANES : (c + 1) * LANES] = found[:, TERMS - 8 :].reshape(LANES, LANES)


WHOLE = pl.BlockSpec(memory_space=pltpu.VMEM)
APART = pl.BlockSpec(memory_space=pltpu.HBM)


def placed(shape, dtype, near=True):
    return pltpu.VMEM(shape, dtype) if near else jax.ShapeDtypeStruct(shape, dtype)


def run(body, outs, *args, name=None, cost=4, specs=None, scratch=()):
    many = isinstance(outs[0][0], tuple)
    return pl.pallas_call(
        body,
        out_shape=tuple(placed(*o) for o in outs) if many else placed(*outs),
        in_specs=specs or [WHOLE] * len(args),
        out_specs=(WHOLE,) * len(outs) if many else WHOLE,
        scratch_shapes=scratch,
        name=name,
        cost_estimate=pl.CostEstimate(
            flops=int(cost * 1e8), bytes_accessed=1 << 20, transcendentals=0
        ),
        compiler_params=pltpu.CompilerParams(vmem_limit_bytes=24 << 20),
    )(*args)


def far(*arrays):
    return [pltpu.with_memory_space_constraint(a, pltpu.HBM) for a in arrays]


def other_core(array):
    return lax.ppermute(array, "core", [(0, 1), (1, 0)])


def exchange(array, axis):
    return lax.all_to_all(array, axis, 0, 0, tiled=True)


def shards(features, conv_weight, reduce_weight, spectral_weight, expand_weight, upstream):
    x = features.reshape(CELLS, 3 * LANES)
    u = upstream.reshape(CELLS, 3 * LANES)
    conv = conv_weight.reshape(9 * LANES, LANES)
    width = width_table()
    height = height_table()
    wide, wide_t = jnp.asarray(width), jnp.asarray(np.ascontiguousarray(width.T))
    tall, tall_t = jnp.asarray(height), jnp.asarray(np.ascontiguousarray(height.T))
    message = ((PEERS, OWNED * 2 * ROWS, LANES), BF)
    cells = ((CELLS, LANES), BF)
    edge = ((3 * BREADTH, LANES), BF)

    spec, hidden, slope, first, last = run(
        forward_rows,
        (message, cells, ((CELLS, LANES), F32), edge, edge),
        *far(x, u, reduce_weight, jnp.asarray(narrow_table())),
        specs=[APART] * 4,
        scratch=(
            pltpu.VMEM((CELLS, 2 * LANES), BF),
            pltpu.VMEM((2 * LANES, LANES), BF),
            pltpu.VMEM((OWNED * PEERS * ROWS, LANES), BF),
            pltpu.SemaphoreType.DMA((7,)),
        ),
        name="forward_rows",
    )
    arrived = exchange(spec, IMAGE)
    forward = [(i, i + 1) for i in range(PEERS - 1)]
    above = lax.ppermute(last, IMAGE, forward)
    below = lax.ppermute(first, IMAGE, [(b, a) for a, b in forward])
    local, conv_terms = run(
        local_part,
        (cells, ((2 * PEERS * CONV, LANES), BF)),
        *(*far(x, u), above, below, *far(conv)),
        specs=[APART, APART, WHOLE, WHOLE, APART],
        scratch=(
            pltpu.VMEM((CELLS, LANES), BF),
            pltpu.VMEM((CELLS, LANES), BF),
            pltpu.VMEM((9 * LANES, LANES), BF),
            pltpu.SemaphoreType.DMA((3,)),
        ),
        name="local_part",
        cost=30,
    )
    sent, flat, mix_slope = run(
        columns_forward,
        (message, ((512, 256), BF), ((512, 256), F32)),
        *(arrived, tall, tall_t, spectral_weight),
        name="columns_forward",
    )
    sent, conv_terms, local = lax.optimization_barrier((sent, conv_terms, local))
    arrived = exchange(sent, IMAGE)
    sent, d_combined, expand = run(
        middle_rows,
        (message, cells, ((2 * LANES, LANES), BF)),
        *(arrived, hidden, u, expand_weight, wide, wide_t),
        name="middle_rows",
    )
    arrived = exchange(sent, IMAGE)
    sent, other = run(
        columns_backward,
        (message, ((2, PEERS, TERMS - 8, LANES), BF)),
        *(arrived, tall, tall_t, spectral_weight, mix_slope, flat, expand, conv_terms),
        name="columns_backward",
    )
    arrived = exchange(sent, IMAGE)
    packed = ((PEERS, TERMS, LANES), BF)
    d_reduce, kept, sent = run(
        last_rows,
        (cells, packed, packed),
        *(arrived, d_combined, slope, x, wide_t, other),
        scratch=(pltpu.VMEM((2, PEERS, 8, LANES), BF),),
        name="last_rows",
    )
    arrived = other_core(sent)
    grad = run(
        global_grad,
        ((CELLS, 3 * LANES), BF, False),
        *(d_reduce, reduce_weight, u, local),
        name="global_grad",
        cost=10,
    )
    sums, grad = lax.optimization_barrier((run(added, packed, kept, arrived, name="added"), grad))
    arrived = exchange(sums, DP)
    sums = run(summed, ((LEVELS, TERMS, LANES), BF), arrived, name="sum_images")
    arrived = exchange(sums, "z")
    sums = run(summed, packed, arrived, name="sum_strips")
    arrived = exchange(sums, DP)
    factor = 1.0 / math.sqrt(PEERS * PEERS * ROWS * BREADTH)
    conv_sum, reduce_sum, spectral_sum, expand_sum = run(
        lambda *refs: unpacked(factor, *refs),
        (
            ((9 * LANES, LANES), F32, False),
            ((256, LANES), F32, False),
            ((256, 256), F32, False),
            ((128, 256), F32, False),
        ),
        *(arrived, other_core(arrived)),
        scratch=(pltpu.VMEM((2, PEERS, TERMS, LANES), BF),),
        name="unpacked",
    )
    return (
        grad.reshape(1, ROWS, BREADTH, 3 * LANES),
        conv_sum.reshape(3, 3, LANES, LANES),
        reduce_sum,
        spectral_sum,
        expand_sum,
    )


def solution(mesh):
    strips = P(DP, IMAGE, None, None)
    return jax.shard_map(
        shards,
        mesh=Mesh(mesh.devices.reshape(LEVELS, 2, SIDE, SIDE), (*IMAGE, *DP)),
        in_specs=(strips, P(), P(), P(), P(), strips),
        out_specs=(strips, P(), P(), P(), P()),
        check_vma=False,
    )
```

time: 140 us -> 121 us (0.86)
  waiting for transfers between devices: 22.4 us -> 5.88 us
  local copies, waits for them, and re-layouts: 10.4 us -> 0.07 us
  blocking collectives: 76.3 us -> 83.2 us
  starting transfers between devices: 15.6 us -> 19.3 us
  Pallas kernels: 13.1 us -> 11.7 us
    all_to_all x3 -> x1, waiting for transfers between devices: 22.4 us -> 0.01 us  [exchange(): return lax.all_to_all(array, axis, 0, 0, tiled=True)]
    unnamed x60 -> x18, local copies, waits for them, and re-layouts: 10.4 us -> 0.07 us
    all_to_all x4 -> x6, blocking collectives: 76.3 us -> 83.2 us  [exchange(): return lax.all_to_all(array, axis, 0, 0, tiled=True)]
    ppermute x2 -> x4, waiting for transfers between devices: 0.01 us -> 5.87 us  [the longest x1 3.64 us: shards(): below = lax.ppermute(first, IMAGE, [(b, a) for a, b in forward])]
    ppermute x2 -> x4, starting transfers between devices: 5 us -> 9.33 us  [the longest x2 3.88 us: other_core(): return lax.ppermute(array, 'core', [(0, 1), (1, 0)])]
    pallas_call x13 -> x11, Pallas kernels: 13.1 us -> 11.7 us  [run(): pl.pallas_call(body, out_shape=tuple((placed(*o) for o in outs)) if many...]
    all_to_all x3 -> x1, starting transfers between devices: 10.6 us -> 9.98 us  [exchange(): return lax.all_to_all(array, axis, 0, 0, tiled=True)]
  transfers between devices with their start and end apart: 5 -> 5, of which waited for: 3 -> 4; matrix products, arithmetic and copies ran while one was open for 0% -> 0% of each run, Pallas kernels for 5% -> 4%
where the time goes in v2:
time: 121 us
  blocking collectives  83.2 us (69%)
  starting transfers between devices  19.3 us (16%)
  Pallas kernels  11.7 us (10%)
  waiting for transfers between devices  5.88 us (5%)
    all_to_all x6, blocking collectives, exchange(): return lax.all_to_all(array, axis, 0, 0, tiled=True)  83.2 us
    pallas_call x11, Pallas kernels, run(): pl.pallas_call(body, out_shape=tuple((placed(*o) for o in outs)) if many...  11.7 us
    all_to_all x1, starting transfers between devices, exchange(): return lax.all_to_all(array, axis, 0, 0, tiled=True)  9.98 us
    ppermute x2, starting transfers between devices, other_core(): return lax.ppermute(array, 'core', [(0, 1), (1, 0)])  3.88 us
    ppermute x1, waiting for transfers between devices, shards(): below = lax.ppermute(first, IMAGE, [(b, a) for a, b in forward])  3.64 us
    ppermute x1, starting transfers between devices, shards(): above = lax.ppermute(last, IMAGE, forward)  3.53 us
  transfers between devices with their start and end apart: 5, of which 4 were waited for; matrix products, arithmetic and copies ran while one was open for 0% of the time, Pallas kernels for 4%

profile of v2, /device:TPU:1, one launch (start us, length us, event | category | flops | bytes accessed | tf_op | source)
XLA Modules:
  0.0 120.9 jit_solution(14023875592132060362)
XLA Ops:
  0.6 2.7 %forward_rows.1 = (bf16[16,64,128]{2,1,0:T(8,128)(2,1)}, bf16[1024,128]{1,0:T(8,128)(2,1)S(1)}, f32[1024,128]{1,0:T(8,128)S(1)}, bf16[384,128]{1,0:T(8,128)(2,1)S(1)}, bf16[384,128]{1,0:T(8,128)(2,1)S(1)}) custom-call(bf16[1024,384]{1,0:T(8,128)(2,1)} %bitcast.5, bf16[1024,384]{1,0:T(8,128)(2,1)} %bitcast.8, bf16[256,128]{1,0:T(8,128)(2,1)} %weight.9, ...), custom_call_target="tpu_custom_call" | custom-call | flops 400000000 | bytes 1048576 | tf_op jit(solution)/shard_map/forward_rows/pallas_call | solution.py:324
  3.3 10.0 %all-to-all-start = ((bf16[16,64,128]{2,1,0:T(8,128)(2,1)}), bf16[16,64,128]{2,1,0:T(8,128)(2,1)S(1)}, u32[]{:S(2)}, u32[]{:S(2)}) async-start(bf16[16,64,128]{2,1,0:T(8,128)(2,1)} %get-tuple-element.32), calls=%async_computation | async-start | bytes 524288 | tf_op jit(solution)/shard_map/all_to_all | solution.py:347
  13.3 3.5 %collective-permute-start = (bf16[384,128]{1,0:T(8,128)(2,1)S(1)}, bf16[384,128]{1,0:T(8,128)(2,1)S(1)}, u32[]{:S(2)}, u32[]{:S(2)}) collective-permute-start(bf16[384,128]{1,0:T(8,128)(2,1)S(1)} %get-tuple-element.34), channel_id=1, source_target_pairs={{0,16},{16,32},{32,48},{48,64},{64,80},{80,96},{96,112},{112,128},... | collective-permute-start | bytes 294920 | tf_op jit(solution)/shard_map/ppermute | solution.py:377
  16.8 1.9 %collective-permute-start.1 = (bf16[384,128]{1,0:T(8,128)(2,1)S(1)}, bf16[384,128]{1,0:T(8,128)(2,1)S(1)}, u32[]{:S(2)}, u32[]{:S(2)}) collective-permute-start(bf16[384,128]{1,0:T(8,128)(2,1)S(1)} %get-tuple-element.35), channel_id=1, source_target_pairs={{16,0},{32,16},{48,32},{64,48},{80,64},{96,80},{112,96},{128,112},... | collective-permute-start | bytes 294920 | tf_op jit(solution)/shard_map/ppermute | solution.py:378
  18.8 0.7 collective-permute-done.above
  19.4 3.6 %collective-permute-done.1.below = bf16[384,128]{1,0:T(8,128)(2,1)S(1)} collective-permute-done((bf16[384,128]{1,0:T(8,128)(2,1)S(1)}, bf16[384,128]{1,0:T(8,128)(2,1)S(1)}, u32[]{:S(2)}, u32[]{:S(2)}) %collective-permute-start.1) | collective-permute-done | bytes 98336 | tf_op jit(solution)/shard_map/ppermute | solution.py:378
  23.1 0.0 copy-start.4
  23.1 0.0 copy-start.5
  23.1 0.0 copy-start.6
  23.1 3.3 %local_part.1 = (bf16[1024,128]{1,0:T(8,128)(2,1)S(1)}, bf16[1280,128]{1,0:T(8,128)(2,1)S(1)}) custom-call(bf16[1024,384]{1,0:T(8,128)(2,1)} %bitcast.6, bf16[1024,384]{1,0:T(8,128)(2,1)} %bitcast.9, bf16[384,128]{1,0:T(8,128)(2,1)S(1)} %collective-permute-done.above, bf16[384,128]{1,0:T(8,128)(2,1)S(1)} %collective-permute-done.1.below, ...), custom_call_target="tpu_custom_call" | custom-call | flops 3000000000 | bytes 1048576 | tf_op jit(solution)/shard_map/local_part/pallas_call | solution.py:324
  26.3 0.0 copy-start.1
  26.4 0.0 all-to-all-done.arrived
  26.4 0.0 copy-done.4
  26.4 0.0 copy-done.5
  26.4 0.0 copy-done.6
  26.4 0.0 copy-start.3
  26.4 0.0 copy-start.8
  26.4 0.7 columns_forward.1
  27.1 0.0 copy-start.2
  27.1 18.3 %all_to_all.35.arrived = bf16[16,64,128]{2,1,0:T(8,128)(2,1)S(1)} all-to-all(bf16[16,64,128]{2,1,0:T(8,128)(2,1)S(1)} %get-tuple-element.38), channel_id=1, replica_groups=mesh['z'=8,'core'=2,'y'=4,'x'=4] {'z','core'}, dimensions={0} | all-to-all | bytes 524288 | tf_op jit(solution)/shard_map/all_to_all | solution.py:347
  45.4 0.0 copy-done.1
  45.4 0.0 copy-done.3
  45.4 0.0 copy-done.8
  45.4 0.0 copy-done.2
  45.4 1.3 %middle_rows.1 = (bf16[16,64,128]{2,1,0:T(8,128)(2,1)S(1)}, bf16[1024,128]{1,0:T(8,128)(2,1)S(1)}, bf16[256,128]{1,0:T(8,128)(2,1)S(1)}) custom-call(bf16[16,64,128]{2,1,0:T(8,128)(2,1)S(1)} %all_to_all.35.arrived, bf16[1024,128]{1,0:T(8,128)(2,1)S(1)} %get-tuple-element.39.hidden, bf16[1024,384]{1,0:T(8,128)(2,1)S(1)} %bitcast.10, ...), custom_call_target="tpu_custom_call" | custom-call | flops 400000000 | bytes 1048576 | tf_op jit(solution)/shard_map/middle_rows/pallas_call | solution.py:324
  46.7 14.4 %all_to_all.36.arrived = bf16[16,64,128]{2,1,0:T(8,128)(2,1)S(1)} all-to-all(bf16[16,64,128]{2,1,0:T(8,128)(2,1)S(1)} %get-tuple-element.40), channel_id=1, replica_groups=mesh['z'=8,'core'=2,'y'=4,'x'=4] {'z','core'}, dimensions={0} | all-to-all | bytes 524288 | tf_op jit(solution)/shard_map/all_to_all | solution.py:347
  61.1 0.0 copy-start
  61.1 0.7 columns_backward.1
  61.8 14.4 %all_to_all.37.arrived = bf16[16,64,128]{2,1,0:T(8,128)(2,1)S(1)} all-to-all(bf16[16,64,128]{2,1,0:T(8,128)(2,1)S(1)} %get-tuple-element.45), channel_id=1, replica_groups=mesh['z'=8,'core'=2,'y'=4,'x'=4] {'z','core'}, dimensions={0} | all-to-all | bytes 524288 | tf_op jit(solution)/shard_map/all_to_all | solution.py:347
  76.1 0.0 copy-done
  76.1 0.0 copy-start.7
  76.1 0.7 last_rows.1
  76.9 0.1 collective-permute-start.2
  77.0 0.0 copy-done.7
  77.0 1.2 global_grad.1
  78.2 0.4 collective-permute-done.2.other
  78.5 0.1 added.1
  78.6 15.3 %all_to_all.38.arrived = bf16[16,72,128]{2,1,0:T(8,128)(2,1)S(1)} all-to-all(bf16[16,72,128]{2,1,0:T(8,128)(2,1)S(1)} %added.1), channel_id=1, replica_groups=mesh['z'=8,'core'=2,'y'=4,'x'=4] {'y','x'}, dimensions={0} | all-to-all | bytes 589824 | tf_op jit(solution)/shard_map/all_to_all | solution.py:347
  93.9 10.4 %all_to_all.39.arrived = bf16[8,72,128]{2,1,0:T(8,128)(2,1)S(1)} all-to-all(bf16[8,72,128]{2,1,0:T(8,128)(2,1)S(1)} %sum_images.1), channel_id=1, replica_groups=mesh['z'=8,'core'=2,'y'=4,'x'=4] {'z'}, dimensions={0} | all-to-all | bytes 294912 | tf_op jit(solution)/shard_map/all_to_all | solution.py:347
  104.4 10.4 %all_to_all.40.refs_0_ = bf16[16,72,128]{2,1,0:T(8,128)(2,1)S(1)} all-to-all(bf16[16,72,128]{2,1,0:T(8,128)(2,1)S(1)} %sum_strips.1), channel_id=1, replica_groups=mesh['z'=8,'core'=2,'y'=4,'x'=4] {'y','x'}, dimensions={0} | all-to-all | bytes 589824 | tf_op jit(solution)/shard_map/all_to_all | solution.py:347
  114.8 3.8 %collective-permute-start.3 = (bf16[16,72,128]{2,1,0:T(8,128)(2,1)S(1)}, bf16[16,72,128]{2,1,0:T(8,128)(2,1)S(1)}, u32[]{:S(2)}, u32[]{:S(2)}) collective-permute-start(bf16[16,72,128]{2,1,0:T(8,128)(2,1)S(1)} %all_to_all.40.refs_0_), channel_id=1, source_target_pairs={{0,16},{16,0},{1,17},{17,1},{2,18},{18,2},{3,19},{19,3},{4,20},{20... | collective-permute-start | bytes 884744 | tf_op jit(solution)/shard_map/ppermute | solution.py:343
  118.6 1.2 collective-permute-done.3.refs_1_
  119.8 1.1 unpacked.1
  (2 shorter events, 0.1 us)
Async XLA Ops:
  3.3 23.1 %all-to-all-start = ((bf16[16,64,128]{2,1,0:T(8,128)(2,1)}), bf16[16,64,128]{2,1,0:T(8,128)(2,1)S(1)}, u32[]{:S(2)}, u32[]{:S(2)}) async-start(bf16[16,64,128]{2,1,0:T(8,128)(2,1)} %get-tuple-element.32), calls=%async_computation | async-start | bytes 524288 | tf_op jit(solution)/shard_map/all_to_all | solution.py:347
  13.3 6.1 %collective-permute-start = (bf16[384,128]{1,0:T(8,128)(2,1)S(1)}, bf16[384,128]{1,0:T(8,128)(2,1)S(1)}, u32[]{:S(2)}, u32[]{:S(2)}) collective-permute-start(bf16[384,128]{1,0:T(8,128)(2,1)S(1)} %get-tuple-element.34), channel_id=1, source_target_pairs={{0,16},{16,32},{32,48},{48,64},{64,80},{80,96},{96,112},{112,128},... | collective-permute-start | bytes 294920 | tf_op jit(solution)/shard_map/ppermute | solution.py:377
  16.8 6.2 %collective-permute-start.1 = (bf16[384,128]{1,0:T(8,128)(2,1)S(1)}, bf16[384,128]{1,0:T(8,128)(2,1)S(1)}, u32[]{:S(2)}, u32[]{:S(2)}) collective-permute-start(bf16[384,128]{1,0:T(8,128)(2,1)S(1)} %get-tuple-element.35), channel_id=1, source_target_pairs={{16,0},{32,16},{48,32},{64,48},{80,64},{96,80},{112,96},{128,112},... | collective-permute-start | bytes 294920 | tf_op jit(solution)/shard_map/ppermute | solution.py:378
  23.1 3.3 %copy-start.4 = (bf16[256,256]{1,0:T(8,128)(2,1)S(1)}, bf16[256,256]{1,0:T(8,128)(2,1)}, u32[]{:S(2)}) copy-start(bf16[256,256]{1,0:T(8,128)(2,1)} %weight.8) | copy-start | bytes 393220
  23.1 3.3 %copy-start.5 = (bf16[256,256]{1,0:T(8,128)(2,1)S(1)}, bf16[256,256]{1,0:T(8,128)(2,1)}, u32[]{:S(2)}) copy-start(bf16[256,256]{1,0:T(8,128)(2,1)} %constant.13.clone.table_t) | copy-start | bytes 393220
  23.1 3.3 %copy-start.6 = (bf16[256,256]{1,0:T(8,128)(2,1)S(1)}, bf16[256,256]{1,0:T(8,128)(2,1)}, u32[]{:S(2)}) copy-start(bf16[256,256]{1,0:T(8,128)(2,1)} %constant.12.clone.table) | copy-start | bytes 393220
  26.3 19.1 %copy-start.1 = (bf16[1,8,128,384]{3,2,1,0:T(8,128)(2,1)S(1)}, bf16[1,8,128,384]{3,2,1,0:T(8,128)(2,1)}, u32[]{:S(2)}) copy-start(bf16[1,8,128,384]{3,2,1,0:T(8,128)(2,1)} %param.16) | copy-start | bytes 2359300
  26.4 19.0 %copy-start.3 = (bf16[512,512]{1,0:T(8,128)(2,1)S(1)}, bf16[512,512]{1,0:T(8,128)(2,1)}, u32[]{:S(2)}) copy-start(bf16[512,512]{1,0:T(8,128)(2,1)} %constant.10.clone.table) | copy-start | bytes 1572868
  26.4 19.0 %copy-start.8 = (bf16[128,256]{1,0:T(8,128)(2,1)S(1)}, bf16[128,256]{1,0:T(8,128)(2,1)}, u32[]{:S(2)}) copy-start(bf16[128,256]{1,0:T(8,128)(2,1)} %weight.7) | copy-start | bytes 196612
  27.1 18.3 %copy-start.2 = (bf16[512,512]{1,0:T(8,128)(2,1)S(1)}, bf16[512,512]{1,0:T(8,128)(2,1)}, u32[]{:S(2)}) copy-start(bf16[512,512]{1,0:T(8,128)(2,1)} %constant.11.clone.table_t) | copy-start | bytes 1572868
  61.1 15.0 %copy-start = (bf16[1,8,128,384]{3,2,1,0:T(8,128)(2,1)S(1)}, bf16[1,8,128,384]{3,2,1,0:T(8,128)(2,1)}, u32[]{:S(2)}) copy-start(bf16[1,8,128,384]{3,2,1,0:T(8,128)(2,1)} %param.11) | copy-start | bytes 2359300
  76.1 0.8 copy-start.7
  76.9 1.7 %collective-permute-start.2 = (bf16[16,72,128]{2,1,0:T(8,128)(2,1)S(1)}, bf16[16,72,128]{2,1,0:T(8,128)(2,1)S(1)}, u32[]{:S(2)}, u32[]{:S(2)}) collective-permute-start(bf16[16,72,128]{2,1,0:T(8,128)(2,1)S(1)} %get-tuple-element.50), channel_id=1, source_target_pairs={{0,16},{16,0},{1,17},{17,1},{2,18},{18,2},{3,19},{19,3},{4,20},{20... | collective-permute-start | bytes 884744 | tf_op jit(solution)/shard_map/ppermute | solution.py:343
  114.8 5.0 %collective-permute-start.3 = (bf16[16,72,128]{2,1,0:T(8,128)(2,1)S(1)}, bf16[16,72,128]{2,1,0:T(8,128)(2,1)S(1)}, u32[]{:S(2)}, u32[]{:S(2)}) collective-permute-start(bf16[16,72,128]{2,1,0:T(8,128)(2,1)S(1)} %all_to_all.40.refs_0_), channel_id=1, source_target_pairs={{0,16},{16,0},{1,17},{17,1},{2,18},{18,2},{3,19},{19,3},{4,20},{20... | collective-permute-start | bytes 884744 | tf_op jit(solution)/shard_map/ppermute | solution.py:343

commit v3 on v2

--- a/solution.py
+++ b/solution.py
@@ -1,3 +1,4 @@
+import functools
 import math
 
 import jax
@@ -159,43 +160,53 @@
     return made
 
 
-def forward_rows(x, u, weight, narrow, spec, hidden, slope, first, last, *scratch):
-    held, near_weight, base, sems = scratch
+def forward_rows(x, u, weight, narrow, spec, hidden, slope, across, within, *scratch):
+    held, near_weight, base, near, sems = scratch
     edge, local = 2 * BREADTH, pl.ds(0, LANES)
-    copies = started(
-        [
-            (narrow, base),
-            (weight, near_weight),
-            (x.at[:, pl.ds(LANES, 2 * LANES)], held),
-            (x.at[pl.ds(0, edge), local], first.at[pl.ds(0, edge)]),
-            (x.at[pl.ds(CELLS - edge, edge), local], last.at[pl.ds(0, edge)]),
-            (u.at[pl.ds(0, BREADTH), local], first.at[pl.ds(edge, BREADTH)]),
-            (u.at[pl.ds(CELLS - BREADTH, BREADTH), local], last.at[pl.ds(edge, BREADTH)]),
-        ],
-        sems,
-    )
-    copies[0].wait()
+    core = lax.axis_index("core")
+    copies = [
+        (x.at[:, pl.ds(LANES, 2 * LANES)], held),
+        (weight, near_weight),
+        (narrow, base),
+    ]
+    for side, target in ((core, across), (1 - core, within)):
+        rows = pl.multiple_of(side * (CELLS - edge), BREADTH)
+        copies.append((x.at[pl.ds(rows, edge), local], target.at[pl.ds(0, edge)]))
+        rows = pl.multiple_of(side * (CELLS - BREADTH), BREADTH)
+        copies.append((u.at[pl.ds(rows, BREADTH), local], target.at[pl.ds(edge, BREADTH)]))
+    copies = started(copies, sems)
+    copies[2].wait()
     row = lax.broadcasted_iota(jnp.int32, (PEERS * OWNED * ROWS, BREADTH), 0) // 2 % HALF
     table = jnp.concatenate(
         [base[...] * (row == g).astype(F32).astype(BF) for g in range(HALF)], axis=1
     )
     copies[1].wait()
-    copies[2].wait()
+    copies[0].wait()
     pre = dot(held[...], near_weight[...])
     sigma = jax.nn.sigmoid(pre)
     low = (pre * sigma).astype(BF)
     hidden[...] = low
-    store_message(spec, to_owners(low, table))
-    slope[...] = slope_of(pre, sigma)
+    for k, block in enumerate(to_owners(low, table)):
+        rows = pl.ds(2 * k * ROWS, 2 * ROWS)
+        near[:, rows] = block
+        copies.append(pltpu.make_async_copy(near.at[:, rows], spec.at[:, rows], sems.at[7 + k]))
+        if k:
+            copies[-2].start()
+    slope[: CELLS // 2] = slope_of(pre, sigma)[: CELLS // 2]
+    copies[-1].start()
+    slope[CELLS // 2 :] = slope_of(pre, sigma)[CELLS // 2 :]
     for copy in copies[3:]:
         copy.wait()
 
 
-def local_part(far_x, far_u, above, below, far_weight, grad, terms, x, u, weight, sems):
+def local_part(far_x, far_u, across, within, far_weight, grad, terms, x, u, weight, sems):
     local = (slice(None), pl.ds(0, LANES))
     copies = started([(far_x.at[local], x), (far_u.at[local], u), (far_weight, weight)], sems)
     for copy in copies:
         copy.wait()
+    upper = lax.axis_index("core") == 0
+    above = jnp.where(upper, across[...], within[...])
+    below = jnp.where(upper, within[...], across[...])
     rows = jnp.concatenate([above[: 2 * BREADTH], x[...], below[: 2 * BREADTH]], axis=0)
 
     def beside(cells):
@@ -296,19 +307,40 @@
     sent[...] = jnp.broadcast_to(total[None], sent.shape)
 
 
-def unpacked(factor, mine, other, conv, reduce, spectral, expand, held):
-    me = lax.axis_index("core")
-    held[me] = mine[...]
-    held[1 - me] = other[...]
+def unpacked(factor, mine, *refs):
+    results, (conv, reduce, spectral, expand), sems = refs[-9:-5], refs[-5:-1], refs[-1]
+    core = lax.axis_index("core")
+    core = core if len(refs) == 9 else 1 - core
+    found = mine[...].astype(F32) * factor
+    reduce[...] = found[:, TERMS - 8 :].reshape(LANES, LANES)
+    conv[...] = found[:, 24 : 24 + CONV].reshape(PEERS * CONV, LANES)
+    spectral[...] = found[:, :16].reshape(256, LANES)
+    expand[...] = found[:, 16:24].reshape(LANES, LANES)
+    begin = pl.multiple_of(core * LANES, LANES)
+    columns = (slice(None), pl.ds(begin, LANES))
+    copies = started(
+        [
+            (reduce, results[1].at[pl.ds(begin, LANES)]),
+            (spectral, results[2].at[columns]),
+            (expand, results[3].at[columns]),
+        ],
+        sems,
+    )
     for c in range(2):
-        found = held[c].astype(F32) * factor
-        spectral[:, c * LANES : (c + 1) * LANES] = found[:, :16].reshape(256, LANES)
-        expand[:, c * LANES : (c + 1) * LANES] = found[:, 16:24].reshape(LANES, LANES)
-        begin = c * PEERS * CONV
-        count = min(PEERS * CONV, 9 * LANES - begin)
-        part = found[:, 24 : 24 + CONV].reshape(PEERS * CONV, LANES)
-        conv[begin : begin + count] = part[:count]
-        reduce[c * LANES : (c + 1) * LANES] = found[:, TERMS - 8 :].reshape(LANES, LANES)
+        count = min(PEERS * CONV, 9 * LANES - c * PEERS * CONV)
+
+        @pl.when(core == c)
+        def _():
+            copy = pltpu.make_async_copy(
+                conv.at[pl.ds(0, count)],
+                results[0].at[pl.ds(c * PEERS * CONV, count)],
+                sems.at[3],
+            )
+            copy.start()
+            copy.wait()
+
+    for copy in copies:
+        copy.wait()
 
 
 WHOLE = pl.BlockSpec(memory_space=pltpu.VMEM)
@@ -319,15 +351,17 @@
     return pltpu.VMEM(shape, dtype) if near else jax.ShapeDtypeStruct(shape, dtype)
 
 
-def run(body, outs, *args, name=None, cost=4, specs=None, scratch=()):
+def run(body, outs, *args, cost=4, specs=None, scratch=(), apart=None, aliases=None):
     many = isinstance(outs[0][0], tuple)
     return pl.pallas_call(
         body,
         out_shape=tuple(placed(*o) for o in outs) if many else placed(*outs),
         in_specs=specs or [WHOLE] * len(args),
-        out_specs=(WHOLE,) * len(outs) if many else WHOLE,
+        out_specs=tuple(APART if apart in ("all", i) else WHOLE for i in range(len(outs)))
+        if many
+        else WHOLE,
+        input_output_aliases=aliases or {},
         scratch_shapes=scratch,
-        name=name,
         cost_estimate=pl.CostEstimate(
             flops=int(cost * 1e8), bytes_accessed=1 << 20, transcendentals=0
         ),
@@ -359,27 +393,28 @@
     cells = ((CELLS, LANES), BF)
     edge = ((3 * BREADTH, LANES), BF)
 
-    spec, hidden, slope, first, last = run(
+    spec, hidden, slope, across, within = run(
         forward_rows,
-        (message, cells, ((CELLS, LANES), F32), edge, edge),
+        ((*message, False), cells, ((CELLS, LANES), F32), edge, edge),
         *far(x, u, reduce_weight, jnp.asarray(narrow_table())),
         specs=[APART] * 4,
         scratch=(
             pltpu.VMEM((CELLS, 2 * LANES), BF),
             pltpu.VMEM((2 * LANES, LANES), BF),
             pltpu.VMEM((OWNED * PEERS * ROWS, LANES), BF),
-            pltpu.SemaphoreType.DMA((7,)),
+            pltpu.VMEM((PEERS, OWNED * 2 * ROWS, LANES), BF),
+            pltpu.SemaphoreType.DMA((7 + OWNED,)),
         ),
-        name="forward_rows",
+        apart=0,
     )
     arrived = exchange(spec, IMAGE)
-    forward = [(i, i + 1) for i in range(PEERS - 1)]
-    above = lax.ppermute(last, IMAGE, forward)
-    below = lax.ppermute(first, IMAGE, [(b, a) for a, b in forward])
+    pairs = [(i, i + 1) for i in range(1, PEERS - 1, 2)]
+    across = lax.ppermute(across, IMAGE, pairs + [(b, a) for a, b in pairs])
+    within = other_core(within)
     local, conv_terms = run(
         local_part,
         (cells, ((2 * PEERS * CONV, LANES), BF)),
-        *(*far(x, u), above, below, *far(conv)),
+        *(*far(x, u), across, within, *far(conv)),
         specs=[APART, APART, WHOLE, WHOLE, APART],
         scratch=(
             pltpu.VMEM((CELLS, LANES), BF),
@@ -387,14 +422,12 @@
             pltpu.VMEM((9 * LANES, LANES), BF),
             pltpu.SemaphoreType.DMA((3,)),
         ),
-        name="local_part",
         cost=30,
     )
     sent, flat, mix_slope = run(
         columns_forward,
         (message, ((512, 256), BF), ((512, 256), F32)),
         *(arrived, tall, tall_t, spectral_weight),
-        name="columns_forward",
     )
     sent, conv_terms, local = lax.optimization_barrier((sent, conv_terms, local))
     arrived = exchange(sent, IMAGE)
@@ -402,14 +435,12 @@
         middle_rows,
         (message, cells, ((2 * LANES, LANES), BF)),
         *(arrived, hidden, u, expand_weight, wide, wide_t),
-        name="middle_rows",
     )
     arrived = exchange(sent, IMAGE)
     sent, other = run(
         columns_backward,
         (message, ((2, PEERS, TERMS - 8, LANES), BF)),
         *(arrived, tall, tall_t, spectral_weight, mix_slope, flat, expand, conv_terms),
-        name="columns_backward",
     )
     arrived = exchange(sent, IMAGE)
     packed = ((PEERS, TERMS, LANES), BF)
@@ -418,34 +449,43 @@
         (cells, packed, packed),
         *(arrived, d_combined, slope, x, wide_t, other),
         scratch=(pltpu.VMEM((2, PEERS, 8, LANES), BF),),
-        name="last_rows",
     )
     arrived = other_core(sent)
     grad = run(
-        global_grad,
-        ((CELLS, 3 * LANES), BF, False),
-        *(d_reduce, reduce_weight, u, local),
-        name="global_grad",
-        cost=10,
-    )
-    sums, grad = lax.optimization_barrier((run(added, packed, kept, arrived, name="added"), grad))
+        global_grad, ((CELLS, 3 * LANES), BF, False), *(d_reduce, reduce_weight, u, local), cost=10
+    )
+    sums, grad = lax.optimization_barrier((run(added, packed, kept, arrived), grad))
     arrived = exchange(sums, DP)
-    sums = run(summed, ((LEVELS, TERMS, LANES), BF), arrived, name="sum_images")
+    sums = run(summed, ((LEVELS, TERMS, LANES), BF), arrived)
     arrived = exchange(sums, "z")
-    sums = run(summed, packed, arrived, name="sum_strips")
+    sums = run(summed, packed, arrived)
     arrived = exchange(sums, DP)
     factor = 1.0 / math.sqrt(PEERS * PEERS * ROWS * BREADTH)
-    conv_sum, reduce_sum, spectral_sum, expand_sum = run(
-        lambda *refs: unpacked(factor, *refs),
-        (
+    halves = dict(
+        outs=(
             ((9 * LANES, LANES), F32, False),
             ((256, LANES), F32, False),
             ((256, 256), F32, False),
             ((128, 256), F32, False),
         ),
-        *(arrived, other_core(arrived)),
-        scratch=(pltpu.VMEM((2, PEERS, TERMS, LANES), BF),),
-        name="unpacked",
+        scratch=(
+            pltpu.VMEM((PEERS * CONV, LANES), F32),
+            pltpu.VMEM((LANES, LANES), F32),
+            pltpu.VMEM((256, LANES), F32),
+            pltpu.VMEM((LANES, LANES), F32),
+            pltpu.SemaphoreType.DMA((4,)),
+        ),
+        apart="all",
+    )
+    unpack = functools.partial(unpacked, factor)
+    own = run(unpack, halves.pop("outs"), arrived, cost=10, **halves)
+    conv_sum, reduce_sum, spectral_sum, expand_sum = run(
+        unpack,
+        tuple((a.shape, a.dtype, False) for a in own),
+        *(other_core(arrived), *own),
+        specs=[WHOLE, *(APART,) * 4],
+        aliases={i + 1: i for i in range(4)},
+        **halves,
     )
     return (
         grad.reshape(1, ROWS, BREADTH, 3 * LANES),

time: 121 us -> 120 us (level)
  starting transfers between devices: 19.3 us -> 17.5 us
    ppermute x2 -> x1, starting transfers between devices: 5.45 us -> 3.53 us  [shards(): across = lax.ppermute(across, IMAGE, pairs + [(b, a) for a, b in pairs])]
    ppermute x2 -> x1, waiting for transfers between devices: 4.3 us -> 5.83 us  [shards(): across = lax.ppermute(across, IMAGE, pairs + [(b, a) for a, b in pairs])]
    pallas_call x11 -> x12, Pallas kernels: 11.7 us -> 12.4 us  [run(): pl.pallas_call(body, out_shape=tuple((placed(*o) for o in outs)) if many...]
    ppermute x2 -> x3, starting transfers between devices: 3.88 us -> 3.98 us  [other_core(): return lax.ppermute(array, 'core', [(0, 1), (1, 0)])]
  transfers between devices with their start and end apart: 5 -> 5, of which waited for: 4 -> 3; matrix products, arithmetic and copies ran while one was open for 0% -> 0% of each run, Pallas kernels for 4% -> 4%
where the time goes in v3:
time: 120 us
  blocking collectives  82.5 us (69%)
  starting transfers between devices  17.5 us (15%)
  Pallas kernels  12.4 us (10%)
  waiting for transfers between devices  6.57 us (5%)
    all_to_all x6, blocking collectives, exchange(): return lax.all_to_all(array, axis, 0, 0, tiled=True)  82.5 us
    pallas_call x12, Pallas kernels, run(): pl.pallas_call(body, out_shape=tuple((placed(*o) for o in outs)) if many...  12.4 us
    all_to_all x1, starting transfers between devices, exchange(): return lax.all_to_all(array, axis, 0, 0, tiled=True)  9.98 us
    ppermute x1, waiting for transfers between devices, shards(): across = lax.ppermute(across, IMAGE, pairs + [(b, a) for a, b in pairs])  5.83 us
    ppermute x3, starting transfers between devices, other_core(): return lax.ppermute(array, 'core', [(0, 1), (1, 0)])  3.98 us
    ppermute x1, starting transfers between devices, shards(): across = lax.ppermute(across, IMAGE, pairs + [(b, a) for a, b in pairs])  3.53 us
  transfers between devices with their start and end apart: 5, of which 3 were waited for; matrix products, arithmetic and copies ran while one was open for 0% of the time, Pallas kernels for 4%

profile of v3, /device:TPU:1, one launch (start us, length us, event | category | flops | bytes accessed | tf_op | source)
XLA Modules:
  0.0 119.9 jit_solution(9711013011512630863)
XLA Ops:
  0.6 2.8 %shard_map.146 = (bf16[16,64,128]{2,1,0:T(8,128)(2,1)}, bf16[1024,128]{1,0:T(8,128)(2,1)S(1)}, f32[1024,128]{1,0:T(8,128)S(1)}, bf16[384,128]{1,0:T(8,128)(2,1)S(1)}, bf16[384,128]{1,0:T(8,128)(2,1)S(1)}) custom-call(bf16[1024,384]{1,0:T(8,128)(2,1)} %bitcast.5, bf16[1024,384]{1,0:T(8,128)(2,1)} %bitcast.8, bf16[256,128]{1,0:T(8,128)(2,1)} %weight.9, ...), custom_call_target="tpu_custom_call" | custom-call | flops 400000000 | bytes 1048576 | tf_op jit(solution)/shard_map/pallas_call | solution.py:356
  3.4 10.0 %all-to-all-start = ((bf16[16,64,128]{2,1,0:T(8,128)(2,1)}), bf16[16,64,128]{2,1,0:T(8,128)(2,1)S(1)}, u32[]{:S(2)}, u32[]{:S(2)}) async-start(bf16[16,64,128]{2,1,0:T(8,128)(2,1)} %get-tuple-element.36), calls=%async_computation | async-start | bytes 524288 | tf_op jit(solution)/shard_map/all_to_all | solution.py:381
  13.4 3.5 %collective-permute-start = (bf16[384,128]{1,0:T(8,128)(2,1)S(1)}, bf16[384,128]{1,0:T(8,128)(2,1)S(1)}, u32[]{:S(2)}, u32[]{:S(2)}) collective-permute-start(bf16[384,128]{1,0:T(8,128)(2,1)S(1)} %get-tuple-element.38), channel_id=1, source_target_pairs={{16,32},{48,64},{80,96},{112,128},{144,160},{176,192},{208,224},{3... | collective-permute-start | bytes 294920 | tf_op jit(solution)/shard_map/ppermute | solution.py:412
  17.0 0.1 collective-permute-start.1
  17.1 5.8 %collective-permute-done.across = bf16[384,128]{1,0:T(8,128)(2,1)S(1)} collective-permute-done((bf16[384,128]{1,0:T(8,128)(2,1)S(1)}, bf16[384,128]{1,0:T(8,128)(2,1)S(1)}, u32[]{:S(2)}, u32[]{:S(2)}) %collective-permute-start) | collective-permute-done | bytes 98336 | tf_op jit(solution)/shard_map/ppermute | solution.py:412
  22.9 0.0 collective-permute-done.1.within
  22.9 0.0 copy-start.4
  22.9 0.0 copy-start.5
  22.9 0.0 copy-start.6
  22.9 3.3 %shard_map.148 = (bf16[1024,128]{1,0:T(8,128)(2,1)S(1)}, bf16[1280,128]{1,0:T(8,128)(2,1)S(1)}) custom-call(bf16[1024,384]{1,0:T(8,128)(2,1)} %bitcast.6, bf16[1024,384]{1,0:T(8,128)(2,1)} %bitcast.9, bf16[384,128]{1,0:T(8,128)(2,1)S(1)} %collective-permute-done.across, bf16[384,128]{1,0:T(8,128)(2,1)S(1)} %collective-permute-done.1.within, ...), custom_call_target="tpu_custom_call" | custom-call | flops 3000000000 | bytes 1048576 | tf_op jit(solution)/shard_map/pallas_call | solution.py:356
  26.2 0.0 copy-start.1
  26.2 0.0 all-to-all-done.arrived
  26.2 0.0 copy-done.4
  26.2 0.0 copy-done.5
  26.2 0.0 copy-done.6
  26.2 0.0 copy-start.3
  26.3 0.0 copy-start.8
  26.3 0.7 shard_map.147
  26.9 0.0 copy-start.2
  27.0 17.7 %all_to_all.35.arrived = bf16[16,64,128]{2,1,0:T(8,128)(2,1)S(1)} all-to-all(bf16[16,64,128]{2,1,0:T(8,128)(2,1)S(1)} %get-tuple-element.42), channel_id=1, replica_groups=mesh['z'=8,'core'=2,'y'=4,'x'=4] {'z','core'}, dimensions={0} | all-to-all | bytes 524288 | tf_op jit(solution)/shard_map/all_to_all | solution.py:381
  44.6 0.0 copy-done.1
  44.6 0.0 copy-done.3
  44.6 0.0 copy-done.8
  44.6 0.0 copy-done.2
  44.6 1.3 %shard_map.149 = (bf16[16,64,128]{2,1,0:T(8,128)(2,1)S(1)}, bf16[1024,128]{1,0:T(8,128)(2,1)S(1)}, bf16[256,128]{1,0:T(8,128)(2,1)S(1)}) custom-call(bf16[16,64,128]{2,1,0:T(8,128)(2,1)S(1)} %all_to_all.35.arrived, bf16[1024,128]{1,0:T(8,128)(2,1)S(1)} %get-tuple-element.43.hidden, bf16[1024,384]{1,0:T(8,128)(2,1)S(1)} %bitcast.10, ...), custom_call_target="tpu_custom_call" | custom-call | flops 400000000 | bytes 1048576 | tf_op jit(solution)/shard_map/pallas_call | solution.py:356
  45.9 14.4 %all_to_all.36.arrived = bf16[16,64,128]{2,1,0:T(8,128)(2,1)S(1)} all-to-all(bf16[16,64,128]{2,1,0:T(8,128)(2,1)S(1)} %get-tuple-element.44), channel_id=1, replica_groups=mesh['z'=8,'core'=2,'y'=4,'x'=4] {'z','core'}, dimensions={0} | all-to-all | bytes 524288 | tf_op jit(solution)/shard_map/all_to_all | solution.py:381
  60.3 0.0 copy-start
  60.3 0.7 shard_map.150
  61.0 14.4 %all_to_all.37.arrived = bf16[16,64,128]{2,1,0:T(8,128)(2,1)S(1)} all-to-all(bf16[16,64,128]{2,1,0:T(8,128)(2,1)S(1)} %get-tuple-element.49), channel_id=1, replica_groups=mesh['z'=8,'core'=2,'y'=4,'x'=4] {'z','core'}, dimensions={0} | all-to-all | bytes 524288 | tf_op jit(solution)/shard_map/all_to_all | solution.py:381
  75.4 0.0 copy-done
  75.4 0.0 copy-start.7
  75.4 0.7 shard_map.151
  76.1 0.1 collective-permute-start.2
  76.2 0.0 copy-done.7
  76.2 1.2 shard_map.153
  77.4 0.4 collective-permute-done.2.other
  77.7 0.1 shard_map.152
  77.8 15.3 %all_to_all.38.arrived = bf16[16,72,128]{2,1,0:T(8,128)(2,1)S(1)} all-to-all(bf16[16,72,128]{2,1,0:T(8,128)(2,1)S(1)} %shard_map.152), channel_id=1, replica_groups=mesh['z'=8,'core'=2,'y'=4,'x'=4] {'y','x'}, dimensions={0} | all-to-all | bytes 589824 | tf_op jit(solution)/shard_map/all_to_all | solution.py:381
  93.1 10.4 %all_to_all.39.arrived = bf16[8,72,128]{2,1,0:T(8,128)(2,1)S(1)} all-to-all(bf16[8,72,128]{2,1,0:T(8,128)(2,1)S(1)} %shard_map.154), channel_id=1, replica_groups=mesh['z'=8,'core'=2,'y'=4,'x'=4] {'z'}, dimensions={0} | all-to-all | bytes 294912 | tf_op jit(solution)/shard_map/all_to_all | solution.py:381
  103.6 10.4 %all_to_all.40.mine = bf16[16,72,128]{2,1,0:T(8,128)(2,1)S(1)} all-to-all(bf16[16,72,128]{2,1,0:T(8,128)(2,1)S(1)} %shard_map.155), channel_id=1, replica_groups=mesh['z'=8,'core'=2,'y'=4,'x'=4] {'y','x'}, dimensions={0} | all-to-all | bytes 589824 | tf_op jit(solution)/shard_map/all_to_all | solution.py:381
  114.0 3.8 %collective-permute-start.3 = (bf16[16,72,128]{2,1,0:T(8,128)(2,1)S(1)}, bf16[16,72,128]{2,1,0:T(8,128)(2,1)S(1)}, u32[]{:S(2)}, u32[]{:S(2)}) collective-permute-start(bf16[16,72,128]{2,1,0:T(8,128)(2,1)S(1)} %all_to_all.40.mine), channel_id=1, source_target_pairs={{0,16},{16,0},{1,17},{17,1},{2,18},{18,2},{3,19},{19,3},{4,20},{20... | collective-permute-start | bytes 884744 | tf_op jit(solution)/shard_map/ppermute | solution.py:377
  117.8 0.8 shard_map.156
  118.7 0.4 collective-permute-done.3.mine
  119.0 0.9 shard_map.157
  (2 shorter events, 0.1 us)
Async XLA Ops:
  3.4 22.8 %all-to-all-start = ((bf16[16,64,128]{2,1,0:T(8,128)(2,1)}), bf16[16,64,128]{2,1,0:T(8,128)(2,1)S(1)}, u32[]{:S(2)}, u32[]{:S(2)}) async-start(bf16[16,64,128]{2,1,0:T(8,128)(2,1)} %get-tuple-element.36), calls=%async_computation | async-start | bytes 524288 | tf_op jit(solution)/shard_map/all_to_all | solution.py:381
  13.4 9.5 %collective-permute-start = (bf16[384,128]{1,0:T(8,128)(2,1)S(1)}, bf16[384,128]{1,0:T(8,128)(2,1)S(1)}, u32[]{:S(2)}, u32[]{:S(2)}) collective-permute-start(bf16[384,128]{1,0:T(8,128)(2,1)S(1)} %get-tuple-element.38), channel_id=1, source_target_pairs={{16,32},{48,64},{80,96},{112,128},{144,160},{176,192},{208,224},{3... | collective-permute-start | bytes 294920 | tf_op jit(solution)/shard_map/ppermute | solution.py:412
  17.0 5.9 %collective-permute-start.1 = (bf16[384,128]{1,0:T(8,128)(2,1)S(1)}, bf16[384,128]{1,0:T(8,128)(2,1)S(1)}, u32[]{:S(2)}, u32[]{:S(2)}) collective-permute-start(bf16[384,128]{1,0:T(8,128)(2,1)S(1)} %get-tuple-element.39), channel_id=1, source_target_pairs={{0,16},{16,0},{1,17},{17,1},{2,18},{18,2},{3,19},{19,3},{4,20},{20... | collective-permute-start | bytes 294920 | tf_op jit(solution)/shard_map/ppermute | solution.py:377
  22.9 3.3 %copy-start.4 = (bf16[256,256]{1,0:T(8,128)(2,1)S(1)}, bf16[256,256]{1,0:T(8,128)(2,1)}, u32[]{:S(2)}) copy-start(bf16[256,256]{1,0:T(8,128)(2,1)} %weight.8) | copy-start | bytes 393220
  22.9 3.3 %copy-start.5 = (bf16[256,256]{1,0:T(8,128)(2,1)S(1)}, bf16[256,256]{1,0:T(8,128)(2,1)}, u32[]{:S(2)}) copy-start(bf16[256,256]{1,0:T(8,128)(2,1)} %constant.13.clone.table_t) | copy-start | bytes 393220
  22.9 3.3 %copy-start.6 = (bf16[256,256]{1,0:T(8,128)(2,1)S(1)}, bf16[256,256]{1,0:T(8,128)(2,1)}, u32[]{:S(2)}) copy-start(bf16[256,256]{1,0:T(8,128)(2,1)} %constant.12.clone.table) | copy-start | bytes 393220
  26.2 18.4 %copy-start.1 = (bf16[1,8,128,384]{3,2,1,0:T(8,128)(2,1)S(1)}, bf16[1,8,128,384]{3,2,1,0:T(8,128)(2,1)}, u32[]{:S(2)}) copy-start(bf16[1,8,128,384]{3,2,1,0:T(8,128)(2,1)} %param.16) | copy-start | bytes 2359300
  26.2 18.4 %copy-start.3 = (bf16[512,512]{1,0:T(8,128)(2,1)S(1)}, bf16[512,512]{1,0:T(8,128)(2,1)}, u32[]{:S(2)}) copy-start(bf16[512,512]{1,0:T(8,128)(2,1)} %constant.10.clone.table) | copy-start | bytes 1572868
  26.3 18.4 %copy-start.8 = (bf16[128,256]{1,0:T(8,128)(2,1)S(1)}, bf16[128,256]{1,0:T(8,128)(2,1)}, u32[]{:S(2)}) copy-start(bf16[128,256]{1,0:T(8,128)(2,1)} %weight.7) | copy-start | bytes 196612
  26.9 17.7 %copy-start.2 = (bf16[512,512]{1,0:T(8,128)(2,1)S(1)}, bf16[512,512]{1,0:T(8,128)(2,1)}, u32[]{:S(2)}) copy-start(bf16[512,512]{1,0:T(8,128)(2,1)} %constant.11.clone.table_t) | copy-start | bytes 1572868
  60.3 15.0 %copy-start = (bf16[1,8,128,384]{3,2,1,0:T(8,128)(2,1)S(1)}, bf16[1,8,128,384]{3,2,1,0:T(8,128)(2,1)}, u32[]{:S(2)}) copy-start(bf16[1,8,128,384]{3,2,1,0:T(8,128)(2,1)} %param.11) | copy-start | bytes 2359300
  75.4 0.8 copy-start.7
  76.1 1.7 %collective-permute-start.2 = (bf16[16,72,128]{2,1,0:T(8,128)(2,1)S(1)}, bf16[16,72,128]{2,1,0:T(8,128)(2,1)S(1)}, u32[]{:S(2)}, u32[]{:S(2)}) collective-permute-start(bf16[16,72,128]{2,1,0:T(8,128)(2,1)S(1)} %get-tuple-element.54), channel_id=1, source_target_pairs={{0,16},{16,0},{1,17},{17,1},{2,18},{18,2},{3,19},{19,3},{4,20},{20... | collective-permute-start | bytes 884744 | tf_op jit(solution)/shard_map/ppermute | solution.py:377
  114.0 5.0 %collective-permute-start.3 = (bf16[16,72,128]{2,1,0:T(8,128)(2,1)S(1)}, bf16[16,72,128]{2,1,0:T(8,128)(2,1)S(1)}, u32[]{:S(2)}, u32[]{:S(2)}) collective-permute-start(bf16[16,72,128]{2,1,0:T(8,128)(2,1)S(1)} %all_to_all.40.mine), channel_id=1, source_target_pairs={{0,16},{16,0},{1,17},{17,1},{2,18},{18,2},{3,19},{19,3},{4,20},{20... | collective-permute-start | bytes 884744 | tf_op jit(solution)/shard_map/ppermute | solution.py:377
